TPU v7x, 8 devices: a whole 2x2x1 slice. The times are simulated.
8 devices in a mesh: dp: 1 (over z), ep: 8 (over y, x, core).
Axes of the slice: x: 2, y: 2, z: 1, core: 2. Of those that a mesh axis runs over, the one named last changes fastest.
Arguments:
- hidden: bfloat16 [256, 7168], P(('dp', 'ep'))
- positions: int32 [256], P(('dp', 'ep'))
- ckv_cache: bfloat16 [256, 64, 512], P(('dp', 'ep'))
- kpe_cache: bfloat16 [256, 64, 64], P(('dp', 'ep'))
- topk_ids: int32 [256, 8], P(('dp', 'ep'))
- attn_gain: bfloat16 [7168], replicated
- w_dq: bfloat16 [7168, 1536], replicated
- q_gain: bfloat16 [1536], replicated
- w_uq: bfloat16 [1536, 3072], replicated
- w_dkv: bfloat16 [7168, 576], replicated
- kv_gain: bfloat16 [512], replicated
- w_uk: bfloat16 [512, 2048], replicated
- w_uv: bfloat16 [512, 2048], replicated
- w_out: bfloat16 [2048, 7168], replicated
- ffn_gain: bfloat16 [7168], replicated
- w_router: bfloat16 [7168, 16], replicated
- w_gate: bfloat16 [16, 7168, 2048], P('ep')
- w_up: bfloat16 [16, 7168, 2048], P('ep')
- w_down: bfloat16 [16, 2048, 7168], P('ep')
- shared_gate: bfloat16 [7168, 2048], replicated
- shared_up: bfloat16 [7168, 2048], replicated
- shared_down: bfloat16 [2048, 7168], replicated
Outputs:
- output 1: bfloat16 [256, 7168], P(('dp', 'ep'))
- output 2: bfloat16 [256, 512], P(('dp', 'ep'))
- output 3: bfloat16 [256, 64], P(('dp', 'ep'))
All inputs are finite; a program needn't handle non-finite values.
Results may differ from a plain program's by a relative error of at most 0.0153635.
Values are sent between devices in bfloat16 or wider.
A program may use at most 1.5 GiB of HBM per device.

v0:
```python
import jax
import jax.numpy as jnp
from jax import lax
from jax.sharding import PartitionSpec as P

NOPE_DIM = 128
ROPE_DIM = 64
VALUE_DIM = 128
QK_DIM = NOPE_DIM + ROPE_DIM
EPSILON = 1e-6
ROUTE_SCALE = 2.5
ROPE_BASE = 10000.0
CAP_FACTOR = 2


def rms_norm(vec, gain):
    vec = vec.astype(jnp.float32)
    scale = lax.rsqrt(jnp.mean(vec * vec, axis=-1, keepdims=True) + EPSILON)
    return vec * scale * gain.astype(jnp.float32)


def rotary(vec, positions):
    half = ROPE_DIM // 2
    freqs = ROPE_BASE ** (-jnp.arange(half).astype(jnp.float32) / half)
    angle = positions.astype(jnp.float32)[..., None] * freqs
    cosine = jnp.cos(angle)
    sine = jnp.sin(angle)
    first = vec[..., :half]
    second = vec[..., half:]
    return jnp.concatenate([first * cosine - second * sine, first * sine + second * cosine], axis=-1)


def attention_block(hidden, positions, ckv_cache, kpe_cache, attn_gain, w_dq, q_gain, w_uq, w_dkv, kv_gain, w_uk, w_uv, w_out):
    tokens = hidden.shape[0]
    kv_rank = w_uk.shape[0]
    heads = w_uk.shape[1] // NOPE_DIM
    cache_len = ckv_cache.shape[1]
    normed = rms_norm(hidden, attn_gain).astype(jnp.bfloat16)
    c_q = rms_norm(jnp.dot(normed, w_dq, preferred_element_type=jnp.float32), q_gain).astype(jnp.bfloat16)
    query = jnp.dot(c_q, w_uq, preferred_element_type=jnp.float32).astype(jnp.bfloat16).reshape(tokens, heads, QK_DIM)
    q_nope = query[:, :, :NOPE_DIM]
    q_rot = rotary(query[:, :, NOPE_DIM:].astype(jnp.float32), positions[:, None]).astype(jnp.bfloat16)
    kv_proj = jnp.dot(normed, w_dkv, preferred_element_type=jnp.float32)
    c_new = rms_norm(kv_proj[:, :kv_rank], kv_gain).astype(jnp.bfloat16)
    k_new = rotary(kv_proj[:, kv_rank:], positions).astype(jnp.bfloat16)
    q_abs = jnp.einsum('thn,chn->thc', q_nope, w_uk.reshape(kv_rank, heads, NOPE_DIM), preferred_element_type=jnp.float32).astype(jnp.bfloat16)
    scale = QK_DIM ** -0.5
    s_cache = (jnp.einsum('thc,tsc->ths', q_abs, ckv_cache, preferred_element_type=jnp.float32) + jnp.einsum('thr,tsr->ths', q_rot, kpe_cache, preferred_element_type=jnp.float32)) * scale
    valid = jnp.arange(cache_len)[None, None, :] < positions[:, None, None]
    s_cache = jnp.where(valid, s_cache, -1e30)
    s_self = (jnp.einsum('thc,tc->th', q_abs, c_new, preferred_element_type=jnp.float32) + jnp.einsum('thr,tr->th', q_rot, k_new, preferred_element_type=jnp.float32)) * scale
    peak = jnp.maximum(jnp.max(s_cache, axis=2), s_self)
    e_cache = jnp.exp(s_cache - peak[:, :, None])
    e_self = jnp.exp(s_self - peak)
    denominator = jnp.sum(e_cache, axis=2) + e_self
    p_cache = (e_cache / denominator[:, :, None]).astype(jnp.bfloat16)
    p_self = (e_self / denominator).astype(jnp.bfloat16)
    context = jnp.einsum('ths,tsc->thc', p_cache, ckv_cache, preferred_element_type=jnp.float32) + p_self.astype(jnp.float32)[:, :, None] * c_new.astype(jnp.float32)[:, None, :]
    heads_out = jnp.einsum('thc,chv->thv', context.astype(jnp.bfloat16), w_uv.reshape(kv_rank, heads, VALUE_DIM), preferred_element_type=jnp.float32).astype(jnp.bfloat16)
    attn_out = jnp.dot(heads_out.reshape(tokens, heads * VALUE_DIM), w_out, preferred_element_type=jnp.float32)
    x_mid = (hidden.astype(jnp.float32) + attn_out).astype(jnp.bfloat16)
    return x_mid, c_new, k_new


def route_weights(u_norm, topk_ids, w_router, capacity):
    experts = w_router.shape[1]
    gates = jax.nn.sigmoid(jnp.dot(u_norm, w_router, preferred_element_type=jnp.float32))
    chosen = jnp.take_along_axis(gates, topk_ids, axis=1)
    weights = ROUTE_SCALE * chosen / jnp.sum(chosen, axis=1, keepdims=True)
    hits = (topk_ids[:, :, None] == jnp.arange(experts)[None, None, :]).astype(jnp.int32)
    per_token = jnp.sum(hits, axis=1)
    before = jnp.cumsum(per_token, axis=0) - per_token
    rank = jnp.sum(hits * before[:, None, :], axis=2)
    keep = rank < capacity
    slots = jnp.where(keep, topk_ids * capacity + rank, -1)
    return jnp.where(keep, weights, 0.0), slots


def expert_block(rows, w_gate, w_up, w_down):
    h_gate = jnp.einsum('slcd,ldf->slcf', rows, w_gate, preferred_element_type=jnp.float32)
    h_up = jnp.einsum('slcd,ldf->slcf', rows, w_up, preferred_element_type=jnp.float32)
    act = (jax.nn.silu(h_gate) * h_up).astype(jnp.bfloat16)
    return jnp.einsum('slcf,lfd->slcd', act, w_down, preferred_element_type=jnp.float32).astype(jnp.bfloat16)


def shared_block(u_norm, shared_gate, shared_up, shared_down):
    h_gate = jnp.dot(u_norm, shared_gate, preferred_element_type=jnp.float32)
    h_up = jnp.dot(u_norm, shared_up, preferred_element_type=jnp.float32)
    act = (jax.nn.silu(h_gate) * h_up).astype(jnp.bfloat16)
    return jnp.dot(act, shared_down, preferred_element_type=jnp.float32).astype(jnp.bfloat16)


def solution(mesh):
    ep_size = mesh.shape['ep']
    batch = P(('dp', 'ep'))
    whole = P()
    by_expert = P('ep')

    def local_step(hidden, positions, ckv_cache, kpe_cache, topk_ids, attn_gain, w_dq, q_gain, w_uq, w_dkv, kv_gain, w_uk, w_uv, w_out, ffn_gain, w_router, w_gate, w_up, w_down, shared_gate, shared_up, shared_down):
        x_mid, c_new, k_new = attention_block(hidden, positions, ckv_cache, kpe_cache, attn_gain, w_dq, q_gain, w_uq, w_dkv, kv_gain, w_uk, w_uv, w_out)
        u_norm = rms_norm(x_mid, ffn_gain).astype(jnp.bfloat16)
        tokens, width = u_norm.shape
        experts = w_router.shape[1]
        local = w_gate.shape[0]
        capacity = (CAP_FACTOR * tokens * topk_ids.shape[1] + experts - 1) // experts
        weights, slots = route_weights(u_norm, topk_ids, w_router, capacity)
        route_mat = jnp.any(slots[:, :, None] == jnp.arange(experts * capacity)[None, None, :], axis=1).astype(jnp.bfloat16)
        outgoing = jnp.einsum('tm,td->md', route_mat, u_norm, preferred_element_type=jnp.float32).astype(jnp.bfloat16)
        incoming = lax.all_to_all(outgoing, 'ep', 0, 0, tiled=True).reshape(ep_size, local, capacity, width)
        results = expert_block(incoming, w_gate, w_up, w_down).reshape(ep_size * local * capacity, width)
        returned = lax.all_to_all(results, 'ep', 0, 0, tiled=True)
        picked = jnp.take(returned, jnp.maximum(slots, 0), axis=0)
        routed = jnp.sum(weights[:, :, None] * picked.astype(jnp.float32), axis=1)
        shared_out = shared_block(u_norm, shared_gate, shared_up, shared_down)
        hidden_out = (x_mid.astype(jnp.float32) + routed + shared_out.astype(jnp.float32)).astype(jnp.bfloat16)
        return hidden_out, c_new, k_new

    in_specs = (batch,) * 5 + (whole,) * 11 + (by_expert,) * 3 + (whole,) * 3
    return jax.shard_map(local_step, mesh=mesh, in_specs=in_specs, out_specs=(batch, batch, batch), check_vma=False)
```

profile of v0, /device:TPU:0, one launch (start us, length us, event | category | flops | bytes accessed | tf_op | source)
XLA Modules:
  0.0 352.3 jit_solution(12733032249507849675)
XLA Ops:
  0.7 0.9 convert_element_type.119
  1.5 1.4 fusion.52
  2.9 9.7 %multiply_reduce_fusion.2 = (f32[32]{0:T(128)S(1)}, f32[32,1536]{1,0:T(8,128)S(1)}) fusion(bf16[7168,1536]{1,0:T(8,128)(2,1)} %param.28, bf16[32,7168]{1,0:T(8,128)(2,1)} %param.22, f32[7168]{0:T(1024)S(1)} %convert_element_type.119, f32[32]{0:T(128)S(1)} %add_rsqrt_fusion.3), kind=kOutput, calls=%fused_computation.76 | convolution fusion | flops 705658880 | bytes 22704384 | tf_op jit(solution)/shard_map/dot_general | solution.py:39
  12.8 1.8 convolution_convert_fusion.2
  14.6 0.3 reshape.200
  15.0 6.0 %fusion.73 = f32[32,576]{1,0:T(8,128)S(1)} fusion(bf16[7168,576]{0,1:T(8,128)(2,1)} %param.31, bf16[32,7168]{1,0:T(8,128)(2,1)S(1)} %copy-done.2, f32[7168]{0:T(1024)S(1)} %convert_element_type.119, f32[32]{0:T(128)S(1)} %add_rsqrt_fusion.3), kind=kOutput, calls=%fused_computation.85 | convolution fusion | flops 265158656 | bytes 8818816 | tf_op jit(solution)/shard_map/dot_general | solution.py:43
  21.2 0.8 fusion.38
  22.0 0.7 fusion.59
  22.8 0.4 fusion.57
  23.4 0.2 subtract_convert_fusion
  23.6 0.2 fusion.80
  23.9 0.5 fusion.91
  24.4 0.2 fusion.66
  24.7 0.5 fusion.34
  25.2 0.8 fusion.46
  26.0 12.1 %multiply_reduce_fusion.1 = (f32[32]{0:T(128)S(1)}, f32[32,7168]{1,0:T(8,128)S(1)}) fusion(bf16[2048,7168]{1,0:T(8,128)(2,1)} %param.35, bf16[16,4,8,128]{3,2,1,0:T(8,128)(2,1)S(1)} %fusion.46, bf16[32,7168]{1,0:T(8,128)(2,1)S(1)} %copy-done.2), kind=kOutput, calls=%fused_computation.57 | convolution fusion | flops 940900352 | bytes 30867584 | tf_op jit(solution)/shard_map/dot_general | solution.py:60
  38.5 0.2 fusion.56
  38.8 2.1 convolution_convert_fusion
  40.9 95.8 %all_to_all.21 = bf16[8,64,7168]{2,1,0:T(8,128)(2,1)} all-to-all(bf16[8,64,7168]{2,1,0:T(8,128)(2,1)S(1)} %bitcast.104), channel_id=1, replica_groups=mesh['dp'=1,'ep'=8] {'ep'}, dimensions={0} | all-to-all | bytes 14680064 | tf_op jit(solution)/shard_map/all_to_all | solution.py:109
  136.7 26.5 %fusion.4 = f32[2,8,32,2048]{3,2,1,0:T(8,128)} fusion(bf16[2,7168,2048]{2,1,0:T(8,128)(2,1)} %param.38, bf16[8,2,32,7168]{3,2,1,0:T(8,128)(2,1)} %bitcast.108), kind=kOutput, calls=%fused_computation.6 | convolution fusion | flops 15032385536 | bytes 70254592 | tf_op jit(solution)/shard_map/slcd,ldf->slcf/dot_general | solution.py:80
  163.2 26.8 %fusion.19 = bf16[8,2,32,2048]{3,2,0,1:T(8,128)(2,1)} fusion(f32[2,8,32,2048]{3,2,1,0:T(8,128)} %fusion.4, bf16[2,7168,2048]{2,1,0:T(8,128)(2,1)} %param.39, bf16[8,2,32,7168]{3,2,1,0:T(8,128)(2,1)} %bitcast.109), kind=kOutput, calls=%fused_computation.22 | convolution fusion | flops 15038676992 | bytes 72351744 | tf_op jit(solution)/shard_map/slcd,ldf->slcf/dot_general | solution.py:81
  190.1 28.3 %fusion.9 = bf16[8,2,32,7168]{3,2,0,1:T(8,128)(2,1)} fusion(bf16[8,2,32,2048]{3,2,0,1:T(8,128)(2,1)} %fusion.19, bf16[2,2048,7168]{2,1,0:T(8,128)(2,1)} %param.40), kind=kOutput, calls=%fused_computation.10 | convolution fusion | flops 15036055552 | bytes 68157440 | tf_op jit(solution)/shard_map/slcf,lfd->slcd/dot_general | solution.py:83
  218.3 6.8 %copy.63 = bf16[8,2,32,7168]{3,2,1,0:T(8,128)(2,1)} copy(bf16[8,2,32,7168]{3,2,0,1:T(8,128)(2,1)} %fusion.9) | data formatting | bytes 14680064 | tf_op jit(solution)/shard_map/convert_element_type | solution.py:83
  225.1 3.7 %all-to-all-start.1 = ((bf16[8,64,7168]{2,1,0:T(8,128)(2,1)}), bf16[8,64,7168]{2,1,0:T(8,128)(2,1)}, u32[]{:S(2)}, u32[]{:S(2)}) async-start(bf16[8,64,7168]{2,1,0:T(8,128)(2,1)} %bitcast.107), calls=%async_computation.1 | async-start | bytes 14680064 | tf_op jit(solution)/shard_map/all_to_all | solution.py:111
  229.2 0.3 fusion.51
  229.5 2.0 gather_fusion.1
  231.9 0.7 pad_maximum_fusion.3
  232.6 12.1 %fusion.89 = f32[32,2048]{1,0:T(8,128)S(1)} fusion(bf16[7168,2048]{1,0:T(8,128)(2,1)} %param.41, f32[32,7168]{1,0:T(8,128)S(1)} %get-tuple-element.20, f32[7168]{0:T(1024)S(1)} %convert_element_type.141, f32[32]{0:T(128)S(1)} %add_rsqrt_fusion), kind=kOutput, calls=%fused_computation.127 | convolution fusion | flops 940212224 | bytes 30568576 | tf_op jit(solution)/shard_map/dot_general | solution.py:87
  244.8 66.8 %all-to-all-done.1 = bf16[8,64,7168]{2,1,0:T(8,128)(2,1)} async-done(((bf16[8,64,7168]{2,1,0:T(8,128)(2,1)}), bf16[8,64,7168]{2,1,0:T(8,128)(2,1)}, u32[]{:S(2)}, u32[]{:S(2)}) %all-to-all-start.1) | async-done | bytes 7340064 | tf_op jit(solution)/shard_map/all_to_all | solution.py:111
  311.6 12.1 %gather_fusion = bf16[256,7168]{1,0:T(8,128)(2,1)} fusion(bf16[512,7168]{1,0:T(8,128)(2,1)} %bitcast.21, s32[1024]{0:T(1024)S(1)} %pad_clamp_fusion), kind=kCustom, calls=%fused_computation | custom fusion | bytes 7341056 | tf_op jit(solution)/shard_map/jit(_take)/gather | solution.py:112
  323.7 6.2 %multiply_reduce_fusion = f32[32,7168]{1,0:T(8,128)} fusion(bf16[256,7168]{1,0:T(8,128)(2,1)} %gather_fusion, f32[32,8]{1,0:T(8,128)S(1)} %copy.58, pred[32,8]{1,0:T(8,128)(4,1)S(1)} %copy.59), kind=kLoop, calls=%fused_computation.18 | loop fusion | flops 7110656 | bytes 4588800 | tf_op jit(solution)/shard_map/reduce_sum | solution.py:113
  329.9 22.1 %fusion.16 = bf16[32,7168]{1,0:T(8,128)(2,1)} fusion(bf16[2048,7168]{1,0:T(8,128)(2,1)} %param.43, bf16[7168,2048]{1,0:T(8,128)(2,1)} %param.42, f32[32,7168]{1,0:T(8,128)S(1)} %get-tuple-element.20, f32[32,7168]{1,0:T(8,128)} %multiply_reduce_fusion, f32[32,2048]{1,0:T(8,128)S(1)} %fusion.89, f32[7168]{0:T(1024)S(1)} %convert_element_type.141, ...), kind=kOutput, calls=%fused_computation.17 | convolution fusion | flops 1881276416 | bytes 61304960 | tf_op jit(solution)/shard_map/dot_general | solution.py:90
  (72 shorter events, 1.8 us)
Async XLA Ops:
  0.6 21.4 %copy-start = (bf16[32,64,512]{2,1,0:T(8,128)(2,1)S(1)}, bf16[32,64,512]{2,1,0:T(8,128)(2,1)}, u32[]{:S(2)}) copy-start(bf16[32,64,512]{2,1,0:T(8,128)(2,1)} %param.24) | copy-start | bytes 6291460
  1.5 11.2 %slice-start = ((s8[9437184]{0:T(1024)(128)(4,1)}), s8[4194304]{0:T(1024)(128)(4,1)S(1)}, s32[]{:S(2)}) async-start(s8[9437184]{0:T(1024)(128)(4,1)} %bitcast.105), calls=%async_computation.2 | async-start | bytes 8388608
  2.9 9.8 %copy-start.9 = (bf16[1536]{0:T(1024)(128)(2,1)S(1)}, bf16[1536]{0:T(1024)(128)(2,1)}, u32[]{:S(2)}) copy-start(bf16[1536]{0:T(1024)(128)(2,1)} %param.29) | copy-start | bytes 9220
  2.9 9.8 %slice-start.1 = ((s8[9437184]{0:T(1024)(128)(4,1)}), s8[4194304]{0:T(1024)(128)(4,1)S(1)}, s32[]{:S(2)}) async-start(s8[9437184]{0:T(1024)(128)(4,1)} %bitcast.105), calls=%async_computation.3 | async-start | bytes 8388608
  2.9 9.8 %slice-start.2 = ((s8[9437184]{0:T(1024)(128)(4,1)}), s8[1048576]{0:T(1024)(128)(4,1)S(1)}, s32[]{:S(2)}) async-start(s8[9437184]{0:T(1024)(128)(4,1)} %bitcast.105), calls=%async_computation.4 | async-start | bytes 2097152
  12.7 2.2 copy-start.11
  12.8 2.3 copy-start.2
  14.5 6.6 %copy-start.10 = (bf16[512]{0:T(512)(128)(2,1)S(1)}, bf16[512]{0:T(512)(128)(2,1)}, u32[]{:S(2)}) copy-start(bf16[512]{0:T(512)(128)(2,1)} %param.32) | copy-start | bytes 3076
  14.9 6.3 %copy-start.3 = (bf16[512,2048]{1,0:T(8,128)(2,1)S(1)}, bf16[512,2048]{1,0:T(8,128)(2,1)}, u32[]{:S(2)}) copy-start(bf16[512,2048]{1,0:T(8,128)(2,1)} %param.33) | copy-start | bytes 6291460
  15.0 8.8 %copy-start.4 = (bf16[32,64,64]{2,1,0:T(8,128)(2,1)S(1)}, bf16[32,64,64]{2,1,0:T(8,128)(2,1)}, u32[]{:S(2)}) copy-start(bf16[32,64,64]{2,1,0:T(8,128)(2,1)} %param.25) | copy-start | bytes 786436
  21.0 4.2 %copy-start.12 = (bf16[512,2048]{1,0:T(8,128)(2,1)S(1)}, bf16[512,2048]{1,0:T(8,128)(2,1)}, u32[]{:S(2)}) copy-start(bf16[512,2048]{1,0:T(8,128)(2,1)} %param.34) | copy-start | bytes 6291460
  22.7 2.4 copy-start.7
  26.0 12.1 %copy-start.6 = (s32[32,8]{0,1:T(8,128)S(1)}, s32[32,8]{0,1:T(8,128)}, u32[]{:S(2)}) copy-start(s32[32,8]{0,1:T(8,128)} %param.26) | copy-start | bytes 3076
  26.0 12.7 %copy-start.8 = (bf16[7168]{0:T(1024)(128)(2,1)S(1)}, bf16[7168]{0:T(1024)(128)(2,1)}, u32[]{:S(2)}) copy-start(bf16[7168]{0:T(1024)(128)(2,1)} %param.36) | copy-start | bytes 43012
  225.1 4.1 %copy-start.5 = (bf16[7168,16]{0,1:T(8,128)(2,1)S(1)}, bf16[7168,16]{0,1:T(8,128)(2,1)}, u32[]{:S(2)}) copy-start(bf16[7168,16]{0,1:T(8,128)(2,1)} %param.37) | copy-start | bytes 688132
  225.1 86.5 %all-to-all-start.1 = ((bf16[8,64,7168]{2,1,0:T(8,128)(2,1)}), bf16[8,64,7168]{2,1,0:T(8,128)(2,1)}, u32[]{:S(2)}, u32[]{:S(2)}) async-start(bf16[8,64,7168]{2,1,0:T(8,128)(2,1)} %bitcast.107), calls=%async_computation.1 | async-start | bytes 14680064 | tf_op jit(solution)/shard_map/all_to_all | solution.py:111
  329.8 22.1 %copy-start.1 = (bf16[32,64,512]{2,1,0:T(8,128)(2,1)S(1)}, bf16[32,64,512]{2,1,0:T(8,128)(2,1)}, u32[]{:S(2)}) copy-start(bf16[32,64,512]{2,1,0:T(8,128)(2,1)} %param.24) | copy-start | bytes 6291460
where the time goes:
time: 357 us; the launch traced here: 352 us
  matrix products  152 us (43%)
  blocking collectives  95.8 us (27%)
  waiting for transfers between devices  66.8 us (19%)
  local copies, waits for them, and re-layouts  22.2 us (6%)
  other arithmetic  10.5 us (3%)
  starting transfers between devices  3.71 us (1%)
    all_to_all x1, blocking collectives, local_step(): lax.all_to_all(outgoing, 'ep', 0, 0, tiled=True)  95.8 us
    all_to_all x1, waiting for transfers between devices, local_step(): returned = lax.all_to_all(results, 'ep', 0, 0, tiled=True)  66.8 us
    dot_general x1, matrix products, expert_block(): jnp.einsum('slcf,lfd->slcd', act, w_down, preferred_element_type=jnp.floa...  28.3 us
    dot_general x1, matrix products, expert_block(): jnp.einsum('slcd,ldf->slcf', rows, w_up, preferred_element_type=jnp.float32)  26.8 us
    dot_general x1, matrix products, expert_block(): jnp.einsum('slcd,ldf->slcf', rows, w_gate, preferred_element_type=jnp.flo...  26.5 us
    dot_general x1, matrix products, shared_block(): jnp.dot(act, shared_down, preferred_element_type=jnp.float32)  22.1 us
    gather x1, local copies, waits for them, and re-layouts, local_step(): picked = jnp.take(returned, jnp.maximum(slots, 0), axis=0)  12.1 us
    dot_general x1, matrix products, shared_block(): h_gate = jnp.dot(u_norm, shared_gate, preferred_element_type=jnp.float32)  12.1 us
  transfers between devices with their start and end apart: 1, of which 1 were waited for; matrix products, arithmetic and copies ran while one was open for 5% of the time, Pallas kernels for 0%

commit v1 on v0

--- a/solution.py
+++ b/solution.py
@@ -1,6 +1,8 @@
 import jax
 import jax.numpy as jnp
 from jax import lax
+from jax.experimental import pallas as pl
+from jax.experimental.pallas import tpu as pltpu
 from jax.sharding import PartitionSpec as P
 
 NOPE_DIM = 128
@@ -11,6 +13,13 @@
 ROUTE_SCALE = 2.5
 ROPE_BASE = 10000.0
 CAP_FACTOR = 2
+MESH = pl.DeviceIdType.MESH
+FF_TILE = 256
+COL_TILE = 512
+DEPTH_A = 3
+DEPTH_B = 8
+LANES = 128
+SIB_LAG = 2
 
 
 def rms_norm(vec, gain):
@@ -62,36 +71,320 @@
     return x_mid, c_new, k_new
 
 
-def route_weights(u_norm, topk_ids, w_router, capacity):
+def gate_table(u_norm, topk_ids, w_router, capacity):
     experts = w_router.shape[1]
+    tokens = u_norm.shape[0]
     gates = jax.nn.sigmoid(jnp.dot(u_norm, w_router, preferred_element_type=jnp.float32))
-    chosen = jnp.take_along_axis(gates, topk_ids, axis=1)
-    weights = ROUTE_SCALE * chosen / jnp.sum(chosen, axis=1, keepdims=True)
-    hits = (topk_ids[:, :, None] == jnp.arange(experts)[None, None, :]).astype(jnp.int32)
-    per_token = jnp.sum(hits, axis=1)
-    before = jnp.cumsum(per_token, axis=0) - per_token
-    rank = jnp.sum(hits * before[:, None, :], axis=2)
-    keep = rank < capacity
-    slots = jnp.where(keep, topk_ids * capacity + rank, -1)
-    return jnp.where(keep, weights, 0.0), slots
-
-
-def expert_block(rows, w_gate, w_up, w_down):
-    h_gate = jnp.einsum('slcd,ldf->slcf', rows, w_gate, preferred_element_type=jnp.float32)
-    h_up = jnp.einsum('slcd,ldf->slcf', rows, w_up, preferred_element_type=jnp.float32)
-    act = (jax.nn.silu(h_gate) * h_up).astype(jnp.bfloat16)
-    return jnp.einsum('slcf,lfd->slcd', act, w_down, preferred_element_type=jnp.float32).astype(jnp.bfloat16)
-
-
-def shared_block(u_norm, shared_gate, shared_up, shared_down):
-    h_gate = jnp.dot(u_norm, shared_gate, preferred_element_type=jnp.float32)
-    h_up = jnp.dot(u_norm, shared_up, preferred_element_type=jnp.float32)
-    act = (jax.nn.silu(h_gate) * h_up).astype(jnp.bfloat16)
-    return jnp.dot(act, shared_down, preferred_element_type=jnp.float32).astype(jnp.bfloat16)
+    hits = jnp.sum((topk_ids[:, :, None] == jnp.arange(experts)[None, None, :]).astype(jnp.float32), axis=1)
+    total = jnp.sum(hits * gates, axis=1, keepdims=True)
+    earlier = (jnp.arange(tokens)[:, None] > jnp.arange(tokens)[None, :]).astype(jnp.float32)
+    before = jnp.dot(earlier, hits, preferred_element_type=jnp.float32)
+    kept = jnp.where(before < capacity, hits, 0.0)
+    table = kept * (ROUTE_SCALE * gates / total)
+    return jnp.pad(table, ((0, 0), (0, LANES - experts)))
+
+
+def moe_kernel(u_ref, xmid_ref, gw_ref, sg, su, sd, wg, wu, wd, out_ref,
+               U, WT, wA, wB, acts, ACT, Pb, R1, RL, RX, RY, so,
+               semA, semB, d_s, d_r, w_s, w_r, sib_s, sib_r, rl_s, rl_r, x_s, x_r, y_s, y_r):
+    tokens, width = u_ref.shape
+    ff = sg.shape[1]
+    n_ff = ff // FF_TILE
+    n_col = width // COL_TILE
+    half = width // 2
+    dp = lax.axis_index('dp')
+    me = lax.axis_index('ep')
+    core = lax.rem(me, 2)
+    chip = me // 2
+    cx = lax.rem(chip, 2)
+    cy = chip // 2
+    kX = cy * 2 + (1 - cx)
+    kY = (1 - cy) * 2 + cx
+    kD = (1 - cy) * 2 + (1 - cx)
+    X = kX * 2 + core
+    Y = kY * 2 + core
+    D = kD * 2 + core
+    sib = chip * 2 + (1 - core)
+
+    def rows(dev):
+        return pl.ds(pl.multiple_of(dev * tokens, tokens), tokens)
+
+    def cols(j, size):
+        return pl.ds(pl.multiple_of(j * size, size), size)
+
+    def rcopy(src, dst, ss, rs, dev):
+        return pltpu.make_async_remote_copy(src_ref=src, dst_ref=dst, send_sem=ss, recv_sem=rs,
+                                            device_id=(dp, dev), device_id_type=MESH)
+
+    def issueA(t):
+        slot = lax.rem(t, DEPTH_A)
+
+        @pl.when(t < n_ff)
+        def _():
+            pltpu.make_async_copy(sg.at[:, cols(t, FF_TILE)], wA.at[slot, :, 0:FF_TILE], semA.at[0, slot]).start()
+            pltpu.make_async_copy(su.at[:, cols(t, FF_TILE)], wA.at[slot, :, FF_TILE:2 * FF_TILE], semA.at[1, slot]).start()
+
+        @pl.when((t >= n_ff) & (t < 3 * n_ff))
+        def _():
+            e = t // n_ff - 1
+            n = lax.rem(t, n_ff)
+            pltpu.make_async_copy(wg.at[e, :, cols(n, FF_TILE)], wA.at[slot, :, 0:FF_TILE], semA.at[0, slot]).start()
+            pltpu.make_async_copy(wu.at[e, :, cols(n, FF_TILE)], wA.at[slot, :, FF_TILE:2 * FF_TILE], semA.at[1, slot]).start()
+
+    def waitA(t):
+        slot = lax.rem(t, DEPTH_A)
+        pltpu.make_async_copy(sg.at[:, 0:FF_TILE], wA.at[slot, :, 0:FF_TILE], semA.at[0, slot]).wait()
+        pltpu.make_async_copy(su.at[:, 0:FF_TILE], wA.at[slot, :, FF_TILE:2 * FF_TILE], semA.at[1, slot]).wait()
+
+    def issueB(b):
+        slot = lax.rem(b, DEPTH_B)
+
+        @pl.when(b < 2 * n_col)
+        def _():
+            pltpu.make_async_copy(wd.at[lax.rem(b, 2), :, cols(b // 2, COL_TILE)], wB.at[slot], semB.at[slot]).start()
+
+        @pl.when((b >= 2 * n_col) & (b < 3 * n_col))
+        def _():
+            pltpu.make_async_copy(sd.at[:, cols(b - 2 * n_col, COL_TILE)], wB.at[slot], semB.at[slot]).start()
+
+    def waitB(b):
+        slot = lax.rem(b, DEPTH_B)
+        pltpu.make_async_copy(sd.at[:, 0:COL_TILE], wB.at[slot], semB.at[slot]).wait()
+
+    for t in range(DEPTH_A):
+        issueA(jnp.int32(t))
+
+    barrier = pltpu.get_barrier_semaphore()
+    for k in range(1, 8):
+        pl.semaphore_signal(barrier, inc=1, device_id=(dp, lax.rem(me + k, 8)), device_id_type=MESH)
+    pl.semaphore_wait(barrier, 7)
+
+    h0 = slice(0, half)
+    h1 = slice(half, width)
+    own = rows(me)
+    rX, rY, rD = rows(X), rows(Y), rows(D)
+    toX0 = rcopy(u_ref.at[:, h0], U.at[own, h0], d_s.at[0], d_r.at[0], X)
+    toY1 = rcopy(u_ref.at[:, h1], U.at[own, h1], d_s.at[1], d_r.at[1], Y)
+    toX1 = rcopy(u_ref.at[:, h1], U.at[own, h1], d_s.at[2], d_r.at[2], X)
+    toY0 = rcopy(u_ref.at[:, h0], U.at[own, h0], d_s.at[3], d_r.at[3], Y)
+    toS = rcopy(u_ref, U.at[own, :], d_s.at[4], d_r.at[4], sib)
+    toX0.start()
+    toY1.start()
+    toX1.start()
+    toY0.start()
+    toS.start()
+    for k in range(1, 8):
+        rcopy(gw_ref, WT.at[own, :], w_s.at[k], w_r.at[k], lax.rem(me + k, 8)).start()
+    WT[own, :] = gw_ref[...]
+    U[own, :] = u_ref[...]
+
+    fromX0 = rcopy(u_ref.at[:, h0], U.at[rX, h0], d_s.at[0], d_r.at[0], X)
+    fromY1 = rcopy(u_ref.at[:, h1], U.at[rY, h1], d_s.at[1], d_r.at[1], Y)
+    fromX1 = rcopy(u_ref.at[:, h1], U.at[rX, h1], d_s.at[2], d_r.at[2], X)
+    fromY0 = rcopy(u_ref.at[:, h0], U.at[rY, h0], d_s.at[3], d_r.at[3], Y)
+    relY = rcopy(U.at[rX, h0], U.at[rX, h0], d_s.at[5], d_r.at[5], Y)
+    relX = rcopy(U.at[rY, h1], U.at[rY, h1], d_s.at[6], d_r.at[6], X)
+    fromD0 = rcopy(U.at[rX, h0], U.at[rD, h0], d_s.at[5], d_r.at[5], Y)
+    fromD1 = rcopy(U.at[rY, h1], U.at[rD, h1], d_s.at[6], d_r.at[6], X)
+    sX = rcopy(U.at[rX, :], U.at[rX, :], d_s.at[7], d_r.at[7], sib)
+    sY = rcopy(U.at[rY, :], U.at[rY, :], d_s.at[8], d_r.at[8], sib)
+    sD = rcopy(U.at[rD, :], U.at[rD, :], d_s.at[9], d_r.at[9], sib)
+
+    def sib_rows(k):
+        return rows(k * 2 + (1 - core))
+
+    def gated(both):
+        g = both[:, 0:FF_TILE]
+        return (g * jax.nn.sigmoid(g) * both[:, FF_TILE:2 * FF_TILE]).astype(jnp.bfloat16)
+
+    def shared_up_step(t, carry):
+        waitA(t)
+        both = jnp.dot(u_ref[...], wA[lax.rem(t, DEPTH_A)], preferred_element_type=jnp.float32)
+        acts[:, cols(t, FF_TILE)] = gated(both)
+        issueA(t + DEPTH_A)
+
+        @pl.when(t == 2)
+        def _():
+            fromX0.wait_recv()
+            relY.start()
+            fromY1.wait_recv()
+            relX.start()
+
+        @pl.when(t == 5)
+        def _():
+            fromX1.wait_recv()
+            sX.start()
+            fromY0.wait_recv()
+            sY.start()
+            for b in range(DEPTH_B):
+                issueB(jnp.int32(b))
+        return carry
+
+    lax.fori_loop(0, n_ff, shared_up_step, 0)
+
+    fromD0.wait_recv()
+    fromD1.wait_recv()
+    sD.start()
+    rcopy(u_ref, U.at[sib_rows(chip), :], d_s.at[4], d_r.at[4], sib).wait_recv()
+    rcopy(U.at[rX, :], U.at[sib_rows(kX), :], d_s.at[7], d_r.at[7], sib).wait_recv()
+    rcopy(U.at[rY, :], U.at[sib_rows(kY), :], d_s.at[8], d_r.at[8], sib).wait_recv()
+    rcopy(U.at[rD, :], U.at[sib_rows(kD), :], d_s.at[9], d_r.at[9], sib).wait_recv()
+    for k in range(1, 8):
+        rcopy(gw_ref, WT.at[rows(lax.rem(me + 8 - k, 8)), :], w_s.at[k], w_r.at[k], lax.rem(me + k, 8)).wait_recv()
+
+    def routed_up_step(t, carry):
+        waitA(t)
+        both = jnp.dot(U[...], wA[lax.rem(t, DEPTH_A)], preferred_element_type=jnp.float32)
+        ACT[t // n_ff - 1, :, cols(lax.rem(t, n_ff), FF_TILE)] = gated(both)
+        issueA(t + DEPTH_A)
+        return carry
+
+    lax.fori_loop(n_ff, 3 * n_ff, routed_up_step, 0)
+
+    for cp in (toX0, toY1, toX1, toY0, toS, relY, relX, sX, sY, sD):
+        cp.wait_send()
+    for k in range(1, 8):
+        rcopy(gw_ref, WT.at[own, :], w_s.at[k], w_r.at[k], lax.rem(me + k, 8)).wait_send()
+
+    lane = lax.broadcasted_iota(jnp.int32, WT.shape, 1)
+    w0 = jnp.sum(jnp.where(lane == 2 * me, WT[...], 0.0), axis=1, keepdims=True)
+    w1 = jnp.sum(jnp.where(lane == 2 * me + 1, WT[...], 0.0), axis=1, keepdims=True)
+
+    def to_sib(j):
+        return rcopy(Pb.at[1 - core, :, :, cols(j, COL_TILE)], R1.at[:, :, cols(j, COL_TILE)], sib_s.at[j], sib_r.at[j], sib)
+
+    def first_leg(j, dev):
+        return rcopy(Pb.at[core, kD, :, cols(j, COL_TILE)], RL.at[:, cols(j, COL_TILE)], rl_s.at[j], rl_r.at[j], dev)
+
+    def last_x(j):
+        return rcopy(Pb.at[core, kX, :, cols(j, COL_TILE)], RX.at[:, cols(j, COL_TILE)], x_s.at[j], x_r.at[j], X)
+
+    def last_y(j):
+        return rcopy(Pb.at[core, kY, :, cols(j, COL_TILE)], RY.at[:, cols(j, COL_TILE)], y_s.at[j], y_r.at[j], Y)
+
+    def chip_sum(j):
+        to_sib(j).wait_recv()
+        Pb[core, :, :, cols(j, COL_TILE)] = Pb[core, :, :, cols(j, COL_TILE)] + R1[:, :, cols(j, COL_TILE)]
+        odd = lax.rem(j, 2)
+
+        @pl.when(odd == 0)
+        def _():
+            first_leg(j, X).start()
+            last_x(j).start()
+
+        @pl.when(odd == 1)
+        def _():
+            first_leg(j, Y).start()
+            last_y(j).start()
+
+    def relay(j):
+        odd = lax.rem(j, 2)
+
+        @pl.when(odd == 0)
+        def _():
+            first_leg(j, X).wait_recv()
+            Pb[core, kY, :, cols(j, COL_TILE)] = Pb[core, kY, :, cols(j, COL_TILE)] + RL[:, cols(j, COL_TILE)]
+            last_y(j).start()
+
+        @pl.when(odd == 1)
+        def _():
+            first_leg(j, Y).wait_recv()
+            Pb[core, kX, :, cols(j, COL_TILE)] = Pb[core, kX, :, cols(j, COL_TILE)] + RL[:, cols(j, COL_TILE)]
+            last_x(j).start()
+
+    def down_step(j, carry):
+        waitB(2 * j)
+        waitB(2 * j + 1)
+        e0 = jnp.dot(ACT[0], wB[lax.rem(2 * j, DEPTH_B)], preferred_element_type=jnp.float32).astype(jnp.bfloat16)
+        e1 = jnp.dot(ACT[1], wB[lax.rem(2 * j + 1, DEPTH_B)], preferred_element_type=jnp.float32).astype(jnp.bfloat16)
+        part = w0 * e0.astype(jnp.float32) + w1 * e1.astype(jnp.float32)
+        for k in range(4):
+            for c in range(2):
+                r = (2 * k + c) * tokens
+                Pb[c, k, :, cols(j, COL_TILE)] = part[r:r + tokens]
+        to_sib(j).start()
+        issueB(2 * j + DEPTH_B)
+        issueB(2 * j + 1 + DEPTH_B)
+
+        @pl.when(j >= SIB_LAG)
+        def _():
+            chip_sum(j - SIB_LAG)
+
+        @pl.when((j >= 5) & (lax.rem(j, 2) == 1))
+        def _():
+            relay((j - 5) // 2)
+        return carry
+
+    lax.fori_loop(0, n_col, down_step, 0)
+    for j in range(n_col - SIB_LAG, n_col):
+        chip_sum(jnp.int32(j))
+    relayed = (n_col - 5 + 1) // 2
+
+    def shared_down_step(j, carry):
+        b = 2 * n_col + j
+        waitB(b)
+        so[:, cols(j, COL_TILE)] = jnp.dot(acts[...], wB[lax.rem(b, DEPTH_B)], preferred_element_type=jnp.float32).astype(jnp.bfloat16)
+        issueB(b + DEPTH_B)
+
+        @pl.when(lax.rem(j, 2) == 0)
+        def _():
+            relay(relayed + j // 2)
+        return carry
+
+    lax.fori_loop(0, n_col, shared_down_step, 0)
+    for j in range(relayed + (n_col + 1) // 2, n_col):
+        relay(jnp.int32(j))
+
+    def finish(j, carry):
+        last_x(j).wait_recv()
+        last_y(j).wait_recv()
+        s = cols(j, COL_TILE)
+        routed = Pb[core, chip, :, s] + RX[:, s] + RY[:, s]
+        out_ref[:, s] = (xmid_ref[:, s].astype(jnp.float32) + routed + so[:, s].astype(jnp.float32)).astype(jnp.bfloat16)
+        to_sib(j).wait_send()
+        first_leg(j, X).wait_send()
+        last_x(j).wait_send()
+        last_y(j).wait_send()
+        return carry
+
+    lax.fori_loop(0, n_col, finish, 0)
+
+
+def moe_call(u_norm, x_mid, table, shared_gate, shared_up, shared_down, w_gate, w_up, w_down):
+    tokens, width = u_norm.shape
+    ff = shared_gate.shape[1]
+    total = 8 * tokens
+    n_col = width // COL_TILE
+    vmem = pl.BlockSpec(memory_space=pltpu.VMEM)
+    hbm = pl.BlockSpec(memory_space=pl.ANY)
+    dma = pltpu.SemaphoreType.DMA
+    bf, f4 = jnp.bfloat16, jnp.float32
+    return pl.pallas_call(
+        moe_kernel,
+        out_shape=jax.ShapeDtypeStruct((tokens, width), bf),
+        in_specs=[vmem] * 3 + [hbm] * 6,
+        out_specs=vmem,
+        scratch_shapes=[
+            pltpu.VMEM((total, width), bf),
+            pltpu.VMEM((total, LANES), f4),
+            pltpu.VMEM((DEPTH_A, width, 2 * FF_TILE), bf),
+            pltpu.VMEM((DEPTH_B, ff, COL_TILE), bf),
+            pltpu.VMEM((tokens, ff), bf),
+            pltpu.VMEM((2, total, ff), bf),
+            pltpu.VMEM((2, 4, tokens, width), f4),
+            pltpu.VMEM((4, tokens, width), f4),
+            pltpu.VMEM((tokens, width), f4),
+            pltpu.VMEM((tokens, width), f4),
+            pltpu.VMEM((tokens, width), f4),
+            pltpu.VMEM((tokens, width), bf),
+            dma((2, DEPTH_A)), dma((DEPTH_B,)), dma((10,)), dma((10,)), dma((8,)), dma((8,)),
+        ] + [dma((n_col,))] * 8,
+        compiler_params=pltpu.CompilerParams(collective_id=0, has_side_effects=True, vmem_limit_bytes=67043328),
+        name='moe_exchange',
+    )(u_norm, x_mid, table, shared_gate, shared_up, shared_down, w_gate, w_up, w_down)
 
 
 def solution(mesh):
-    ep_size = mesh.shape['ep']
     batch = P(('dp', 'ep'))
     whole = P()
     by_expert = P('ep')
@@ -99,20 +392,11 @@
     def local_step(hidden, positions, ckv_cache, kpe_cache, topk_ids, attn_gain, w_dq, q_gain, w_uq, w_dkv, kv_gain, w_uk, w_uv, w_out, ffn_gain, w_router, w_gate, w_up, w_down, shared_gate, shared_up, shared_down):
         x_mid, c_new, k_new = attention_block(hidden, positions, ckv_cache, kpe_cache, attn_gain, w_dq, q_gain, w_uq, w_dkv, kv_gain, w_uk, w_uv, w_out)
         u_norm = rms_norm(x_mid, ffn_gain).astype(jnp.bfloat16)
-        tokens, width = u_norm.shape
+        tokens = u_norm.shape[0]
         experts = w_router.shape[1]
-        local = w_gate.shape[0]
         capacity = (CAP_FACTOR * tokens * topk_ids.shape[1] + experts - 1) // experts
-        weights, slots = route_weights(u_norm, topk_ids, w_router, capacity)
-        route_mat = jnp.any(slots[:, :, None] == jnp.arange(experts * capacity)[None, None, :], axis=1).astype(jnp.bfloat16)
-        outgoing = jnp.einsum('tm,td->md', route_mat, u_norm, preferred_element_type=jnp.float32).astype(jnp.bfloat16)
-        incoming = lax.all_to_all(outgoing, 'ep', 0, 0, tiled=True).reshape(ep_size, local, capacity, width)
-        results = expert_block(incoming, w_gate, w_up, w_down).reshape(ep_size * local * capacity, width)
-        returned = lax.all_to_all(results, 'ep', 0, 0, tiled=True)
-        picked = jnp.take(returned, jnp.maximum(slots, 0), axis=0)
-        routed = jnp.sum(weights[:, :, None] * picked.astype(jnp.float32), axis=1)
-        shared_out = shared_block(u_norm, shared_gate, shared_up, shared_down)
-        hidden_out = (x_mid.astype(jnp.float32) + routed + shared_out.astype(jnp.float32)).astype(jnp.bfloat16)
+        table = gate_table(u_norm, topk_ids, w_router, capacity)
+        hidden_out = moe_call(u_norm, x_mid, table, shared_gate, shared_up, shared_down, w_gate, w_up, w_down)
         return hidden_out, c_new, k_new
 
     in_specs = (batch,) * 5 + (whole,) * 11 + (by_expert,) * 3 + (whole,) * 3

time: 357 us -> 157 us (0.44); the launches traced: 352 us -> 157 us
  matrix products: 152 us -> 37.3 us
  Pallas kernels: 0 us -> 102 us
  blocking collectives: 95.8 us -> 0 us
  waiting for transfers between devices: 66.8 us -> 0 us
  local copies, waits for them, and re-layouts: 22.2 us -> 5.03 us
  starting transfers between devices: 3.71 us -> 0 us
    dot_general x7 -> x2, matrix products: 118 us -> 0.5 us  [the longest x1 0.38 us: gate_table(): jnp.dot(u_norm, w_router, preferred_element_type=jnp.float32)]
    pallas_call x0 -> x1, Pallas kernels: none -> 102 us  [moe_call(): pl.pallas_call(moe_kernel, out_shape=jax.ShapeDtypeStruct((tokens, width)...]
    all_to_all x1 -> x0, blocking collectives: 95.8 us -> none  [local_step(): lax.all_to_all(outgoing, 'ep', 0, 0, tiled=True)]
    all_to_all x1 -> x0, waiting for transfers between devices: 66.8 us -> none  [local_step(): returned = lax.all_to_all(results, 'ep', 0, 0, tiled=True)]
    gather x6 -> x0, local copies, waits for them, and re-layouts: 14.5 us -> none  [the longest x1 12.1 us: local_step(): picked = jnp.take(returned, jnp.maximum(slots, 0), axis=0)]
    convert_element_type x1 -> x0, local copies, waits for them, and re-layouts: 6.76 us -> none  [expert_block(): jnp.einsum('slcf,lfd->slcd', act, w_down, preferred_element_type=jnp.floa...]
    reduce_sum x4 -> x1, other arithmetic: 6.22 us -> 0.7 us  [gate_table(): jnp.sum((topk_ids[:, :, None] == jnp.arange(experts)[None, None, :]).asty...]
    all_to_all x1 -> x0, starting transfers between devices: 3.71 us -> none  [local_step(): returned = lax.all_to_all(results, 'ep', 0, 0, tiled=True)]
  transfers between devices with their start and end apart: 1 -> 0, of which waited for: 1 -> 0; matrix products, arithmetic and copies ran while one was open for 5% -> 0% of each run, Pallas kernels for 0% -> 0%
where the time goes in v1:
time: 157 us
  Pallas kernels  102 us (65%)
  matrix products  37.3 us (24%)
  other arithmetic  11.8 us (8%)
  local copies, waits for them, and re-layouts  5.03 us (3%)
    pallas_call x1, Pallas kernels, moe_call(): pl.pallas_call(moe_kernel, out_shape=jax.ShapeDtypeStruct((tokens, width)...  102 us
    dot_general x1, matrix products, attention_block(): jnp.dot(heads_out.reshape(tokens, heads * VALUE_DIM), w_out, preferred_el...  12.3 us
    dot_general x1, matrix products, attention_block(): jnp.dot(normed, w_dq, preferred_element_type=jnp.float32)  9.6 us
    dot_general x1, matrix products, attention_block(): kv_proj = jnp.dot(normed, w_dkv, preferred_element_type=jnp.float32)  6.09 us
    unnamed x33, local copies, waits for them, and re-layouts  3.41 us
    convert_element_type x4, other arithmetic, rms_norm(): return vec * scale * gain.astype(jnp.float32)  3.41 us

profile of v1, /device:TPU:0, one launch (start us, length us, event | category | flops | bytes accessed | tf_op | source)
XLA Modules:
  0.0 156.9 jit_solution(6274085901954379410)
XLA Ops:
  0.6 0.7 convert_element_type.101
  1.4 1.2 fusion.30
  2.6 0.7 convert_element_type.103
  3.3 1.3 iota_compare_fusion.2
  4.6 0.7 convert_reduce_fusion
  5.3 0.7 convert_element_type.95
  6.0 0.7 copy.59
  6.7 0.7 convert_element_type.93
  7.4 1.3 convert_element_type.114
  8.7 6.1 %fusion.44 = f32[32,576]{1,0:T(8,128)S(1)} fusion(bf16[7168,576]{0,1:T(8,128)(2,1)} %param.31, bf16[32,7168]{1,0:T(8,128)(2,1)} %param.22, f32[7168]{0:T(1024)S(1)} %convert_element_type.93, f32[32]{0:T(128)S(1)} %add_rsqrt_fusion.3), kind=kOutput, calls=%fused_computation.54 | convolution fusion | flops 265158656 | bytes 8818816 | tf_op jit(solution)/shard_map/dot_general | solution.py:52
  15.0 0.7 subtract_convert_fusion.1
  15.7 0.7 fusion.70
  16.4 0.7 pad_maximum_fusion.3
  17.1 0.7 fusion.58
  17.8 9.6 %multiply_reduce_fusion = (f32[32]{0:T(128)S(1)}, f32[32,1536]{1,0:T(8,128)S(1)}) fusion(bf16[7168,1536]{1,0:T(8,128)(2,1)} %param.28, bf16[32,7168]{1,0:T(8,128)(2,1)S(1)} %copy-done, f32[7168]{0:T(1024)S(1)} %convert_element_type.93, f32[32]{0:T(128)S(1)} %add_rsqrt_fusion.3), kind=kOutput, calls=%fused_computation.46 | convolution fusion | flops 705658880 | bytes 22704384 | tf_op jit(solution)/shard_map/dot_general | solution.py:48
  27.4 1.8 %convolution_convert_fusion = bf16[32,3072]{1,0:T(8,128)(2,1)S(1)} fusion(bf16[1536,3072]{1,0:T(8,128)(2,1)S(1)} %bitcast.50, f32[32,1536]{1,0:T(8,128)S(1)} %get-tuple-element.14, f32[1536]{0:T(1024)S(1)} %convert_element_type.95, f32[32]{0:T(128)S(1)} %add_rsqrt_fusion.2), kind=kOutput, calls=%fused_computation.2 | convolution fusion | flops 302235648 | bytes 9836672 | tf_op jit(solution)/shard_map/dot_general | solution.py:49
  29.2 0.3 reshape.152
  29.6 1.0 subtract_convert_fusion
  30.6 0.9 fusion.51
  31.6 2.4 %fusion.11 = bf16[32,16,512]{2,0,1:T(8,128)(2,1)S(1)} fusion(bf16[32,16,128]{2,1,0:T(8,128)(2,1)S(1)} %slice.31, bf16[512,2048]{1,0:T(8,128)(2,1)} %param.33), kind=kOutput, calls=%fused_computation.14 | convolution fusion | flops 67371008 | bytes 2752512 | tf_op jit(solution)/shard_map/thn,chn->thc/dot_general | solution.py:55
  34.0 1.2 fusion.34
  35.2 0.7 fusion.36
  35.9 0.5 fusion.59
  36.7 0.5 fusion.7
  37.2 0.8 fusion.19
  38.1 12.3 %fusion.27 = (f32[32]{0:T(128)S(1)}, bf16[32,7168]{1,0:T(8,128)(2,1)S(1)}) fusion(bf16[2048,7168]{1,0:T(8,128)(2,1)} %param.35, bf16[16,4,8,128]{3,2,1,0:T(8,128)(2,1)S(1)} %fusion.19, bf16[32,7168]{1,0:T(8,128)(2,1)S(1)} %copy-done), kind=kOutput, calls=%fused_computation.29 | convolution fusion | flops 940900352 | bytes 30408832 | tf_op jit(solution)/shard_map/dot_general | solution.py:69
  50.4 0.8 copy-done.2
  51.4 0.8 copy-done.3
  52.1 0.4 multiply_reduce_fusion.2
  52.6 0.6 pad.4.gw_ref
  53.3 101.8 %moe_exchange.1 = bf16[32,7168]{1,0:T(8,128)(2,1)} custom-call(bf16[32,7168]{1,0:T(8,128)(2,1)} %copy-done.3, bf16[32,7168]{1,0:T(8,128)(2,1)} %copy-done.2, f32[32,128]{1,0:T(8,128)} %pad.4.gw_ref, bf16[7168,2048]{1,0:T(8,128)(2,1)} %sg.1, bf16[7168,2048]{1,0:T(8,128)(2,1)} %su.1, bf16[2048,7168]{1,0:T(8,128)(2,1)} %sd.1, bf16[2,7168,2048]{2,1,0:T(8,128)(2,1)} %wg.1, ...), custom_call_target="tpu_custom_call" | custom-call | tf_op jit(solution)/shard_map/moe_exchange/pallas_call | solution.py:362
  155.1 1.8 %copy.109 = bf16[32,7168]{1,0:T(8,128)(2,1)} copy(bf16[32,7168]{1,0:T(8,128)(2,1)} %moe_exchange.1) | data formatting | bytes 917504
  (44 shorter events, 0.9 us)
Async XLA Ops:
  0.6 17.1 %copy-start = (bf16[32,7168]{1,0:T(8,128)(2,1)S(1)}, bf16[32,7168]{1,0:T(8,128)(2,1)}, u32[]{:S(2)}) copy-start(bf16[32,7168]{1,0:T(8,128)(2,1)} %param.22) | copy-start | bytes 1376260
  5.3 9.6 %copy-start.7 = (f32[32,16]{0,1:T(8,128)}, f32[32,16]{0,1:T(8,128)S(1)}, u32[]{:S(2)}) copy-start(f32[32,16]{0,1:T(8,128)S(1)} %convert_reduce_fusion) | copy-start | bytes 6148
  8.7 18.7 %slice-start = ((s8[9437184]{0:T(1024)(128)(4,1)}), s8[4194304]{0:T(1024)(128)(4,1)S(1)}, s32[]{:S(2)}) async-start(s8[9437184]{0:T(1024)(128)(4,1)} %bitcast.49), calls=%async_computation | async-start | bytes 8388608
  17.8 9.6 %slice-start.1 = ((s8[9437184]{0:T(1024)(128)(4,1)}), s8[4194304]{0:T(1024)(128)(4,1)S(1)}, s32[]{:S(2)}) async-start(s8[9437184]{0:T(1024)(128)(4,1)} %bitcast.49), calls=%async_computation.1 | async-start | bytes 8388608
  17.8 9.6 %slice-start.2 = ((s8[9437184]{0:T(1024)(128)(4,1)}), s8[1048576]{0:T(1024)(128)(4,1)S(1)}, s32[]{:S(2)}) async-start(s8[9437184]{0:T(1024)(128)(4,1)} %bitcast.49), calls=%async_computation.2 | async-start | bytes 2097152
  27.4 7.8 %copy-start.1 = (bf16[32,64,512]{2,1,0:T(8,128)(2,1)S(1)}, bf16[32,64,512]{2,1,0:T(8,128)(2,1)}, u32[]{:S(2)}) copy-start(bf16[32,64,512]{2,1,0:T(8,128)(2,1)} %param.24) | copy-start | bytes 6291460
  29.2 6.6 %copy-start.4 = (bf16[32,64,64]{2,1,0:T(8,128)(2,1)S(1)}, bf16[32,64,64]{2,1,0:T(8,128)(2,1)}, u32[]{:S(2)}) copy-start(bf16[32,64,64]{2,1,0:T(8,128)(2,1)} %param.25) | copy-start | bytes 786436
  29.5 6.3 %copy-start.9 = (pred[32,64]{1,0:T(8,128)(4,1)S(1)}, pred[32,64]{1,0:T(8,128)(4,1)}, u32[]{:S(2)}) copy-start(pred[32,64]{1,0:T(8,128)(4,1)} %iota_compare_fusion.2) | copy-start | bytes 6148
  29.6 7.1 %copy-start.5 = (f32[32,512]{1,0:T(8,128)S(1)}, f32[32,512]{1,0:T(8,128)}, u32[]{:S(2)}) copy-start(f32[32,512]{1,0:T(8,128)} %get-tuple-element.3) | copy-start | bytes 196612
  29.6 7.6 %copy-start.11 = (bf16[512,2048]{1,0:T(8,128)(2,1)S(1)}, bf16[512,2048]{1,0:T(8,128)(2,1)}, u32[]{:S(2)}) copy-start(bf16[512,2048]{1,0:T(8,128)(2,1)} %param.34) | copy-start | bytes 6291460
  38.0 13.2 %copy-start.6 = (f32[7168]{0:T(1024)S(1)}, f32[7168]{0:T(1024)}, u32[]{:S(2)}) copy-start(f32[7168]{0:T(1024)} %convert_element_type.114) | copy-start | bytes 86020
  38.0 14.1 %copy-start.10 = (f32[32,16]{1,0:T(8,128)S(1)}, f32[32,16]{1,0:T(8,128)}, u32[]{:S(2)}) copy-start(f32[32,16]{1,0:T(8,128)} %copy.59) | copy-start | bytes 6148
  38.0 14.1 %copy-start.12 = (bf16[7168,16]{0,1:T(8,128)(2,1)S(1)}, bf16[7168,16]{0,1:T(8,128)(2,1)}, u32[]{:S(2)}) copy-start(bf16[7168,16]{0,1:T(8,128)(2,1)} %param.37) | copy-start | bytes 688132
  38.1 14.5 %copy-start.8 = (f32[32,16]{0,1:T(8,128)S(1)}, f32[32,16]{0,1:T(8,128)}, u32[]{:S(2)}) copy-start(f32[32,16]{0,1:T(8,128)} %copy-done.7) | copy-start | bytes 6148
  50.4 0.8 copy-start.2
  51.4 0.8 copy-start.3

commit v2 on v0

v2 whole, which is shorter than its diff:
```python
import jax
import jax.numpy as jnp
import numpy as np
from jax import lax
from jax.experimental import pallas as pl
from jax.experimental.pallas import tpu as pltpu
from jax.sharding import PartitionSpec as P

NOPE_DIM = 128
ROPE_DIM = 64
VALUE_DIM = 128
QK_DIM = NOPE_DIM + ROPE_DIM
EPSILON = 1e-6
ROUTE_SCALE = 2.5
ROPE_BASE = 10000.0
CAP_FACTOR = 2
MESH = pl.DeviceIdType.MESH
HEADS = 16
CACHE = 64
FF_TILE = 256
COL_TILE = 512
Q_TILE = 2 * QK_DIM
GROUP = 1024
KV_ROWS = 1024
DEPTH_A = 3
DEPTH_B = 7
LANES = 128
SCALE_LANE = 64
SIB_LAG = 2
SIB_SLOTS = 4
EARLY = 5
SUB = 8
BF = jnp.bfloat16
F4 = jnp.float32


def layer_kernel(pos_ref, topk_ref, freq_ref, ag_ref, qg_ref, kg_ref, fg_ref,
                 hidden, ckv, kpe, dq, uq, dkv, uk, uv, wo, router, sg, su, sd, wg, wu, wd,
                 out_ref, cnew_ref, knew_ref,
                 U, WT, wA, wB, wD, wR, kp, kvs, hid, xm, cq, QN, QA, QR, CTX, O, acts, ACT, Pm, Ps, R1, RL, RX, RY,
                 semA, semB, semD, semM, px_s, px_r, py_s, py_r, pr_s, pr_r, d_s, d_r, w_s, w_r,
                 sib_s, sib_r, rl_s, rl_r, x_s, x_r, y_s, y_r):
    tokens, width = hid.shape
    ff = sg.shape[1]
    rank = uk.shape[0]
    q_rank = cq.shape[1]
    n_ff = ff // FF_TILE
    n_col = width // COL_TILE
    n_grp = width // GROUP
    n_q = uq.shape[1] // Q_TILE
    n_dq = q_rank // COL_TILE
    dp = lax.axis_index('dp')
    me = lax.axis_index('ep')
    core = lax.rem(me, 2)
    chip = me // 2
    cx = lax.rem(chip, 2)
    cy = chip // 2
    kX = cy * 2 + (1 - cx)
    kY = (1 - cy) * 2 + cx
    kD = (1 - cy) * 2 + (1 - cx)
    X = kX * 2 + core
    Y = kY * 2 + core
    sib = chip * 2 + (1 - core)

    def rows(block):
        return pl.ds(pl.multiple_of(block * tokens, tokens), tokens)

    def cols(j, size):
        return pl.ds(pl.multiple_of(j * size, size), size)

    def copy(src, dst, sem):
        return pltpu.make_async_copy(src, dst, sem)

    def rcopy(src, dst, ss, rs, dev):
        return pltpu.make_async_remote_copy(src_ref=src, dst_ref=dst, send_sem=ss, recv_sem=rs,
                                            device_id=(dp, dev), device_id_type=MESH)

    def dot(a, b):
        return jnp.dot(a, b, preferred_element_type=F4)

    def dot_t(a, b):
        return lax.dot_general(a, b, (((1,), (1,)), ((), ())), preferred_element_type=F4)

    A_S0 = n_dq
    A_R = A_S0 + EARLY
    A_S1 = A_R + 2 * n_ff
    A_END = A_S1 + n_ff - EARLY

    def issueA(t):
        slot = lax.rem(t, DEPTH_A)

        def pair(left, right):
            copy(left, wA.at[slot, :, 0:FF_TILE], semA.at[0, slot]).start()
            copy(right, wA.at[slot, :, FF_TILE:2 * FF_TILE], semA.at[1, slot]).start()

        @pl.when(t < n_dq)
        def _():
            copy(dq.at[:, cols(t, COL_TILE)], wA.at[slot], semA.at[0, slot]).start()

        @pl.when((t >= A_S0) & (t < A_R))
        def _():
            n = t - A_S0
            pair(sg.at[:, cols(n, FF_TILE)], su.at[:, cols(n, FF_TILE)])

        @pl.when((t >= A_R) & (t < A_S1))
        def _():
            e = (t - A_R) // n_ff
            n = lax.rem(t - A_R, n_ff)
            pair(wg.at[e, :, cols(n, FF_TILE)], wu.at[e, :, cols(n, FF_TILE)])

        @pl.when((t >= A_S1) & (t < A_END))
        def _():
            n = t - A_S1 + EARLY
            pair(sg.at[:, cols(n, FF_TILE)], su.at[:, cols(n, FF_TILE)])

    def wait_whole(t):
        slot = lax.rem(t, DEPTH_A)
        copy(dq.at[:, 0:COL_TILE], wA.at[slot], semA.at[0, slot]).wait()

    def wait_pair(t):
        slot = lax.rem(t, DEPTH_A)
        copy(sg.at[:, 0:FF_TILE], wA.at[slot, :, 0:FF_TILE], semA.at[0, slot]).wait()
        copy(su.at[:, 0:FF_TILE], wA.at[slot, :, FF_TILE:2 * FF_TILE], semA.at[1, slot]).wait()

    B_UK = n_q
    B_CKV = n_q + 1
    B_UV = n_q + 2
    B_O = n_q + 3
    B_D = B_O + n_col
    B_S = B_D + 2 * n_col
    B_END = B_S + n_col

    def issueB(b):
        slot = lax.rem(b, DEPTH_B)

        def blocks(src):
            for q in range(4):
                copy(src.at[:, q * COL_TILE:(q + 1) * COL_TILE], wB.at[slot, q * rank:(q + 1) * rank, :], semB.at[slot]).start()

        @pl.when(b < n_q)
        def _():
            copy(uq.at[:, cols(b, Q_TILE)], wB.at[slot, 0:q_rank, 0:Q_TILE], semB.at[slot]).start()

        @pl.when(b == B_UK)
        def _():
            blocks(uk)

        @pl.when(b == B_CKV)
        def _():
            copy(ckv, wB.at[slot], semB.at[slot]).start()

        @pl.when(b == B_UV)
        def _():
            blocks(uv)

        @pl.when((b >= B_O) & (b < B_D))
        def _():
            copy(wo.at[:, cols(b - B_O, COL_TILE)], wB.at[slot], semB.at[slot]).start()

        @pl.when((b >= B_D) & (b < B_S))
        def _():
            copy(wd.at[lax.rem(b - B_D, 2), :, cols((b - B_D) // 2, COL_TILE)], wB.at[slot], semB.at[slot]).start()

        @pl.when((b >= B_S) & (b < B_END))
        def _():
            copy(sd.at[:, cols(b - B_S, COL_TILE)], wB.at[slot], semB.at[slot]).start()

    def waitB(b):
        slot = lax.rem(b, DEPTH_B)
        copy(sd.at[:, 0:COL_TILE], wB.at[slot], semB.at[slot]).wait()

    n_kv = width // KV_ROWS

    def kv_copy(c):
        slot = lax.rem(c, 2)
        return copy(dkv.at[:, cols(c, KV_ROWS)], wD.at[slot], semD.at[slot])

    copy(hidden, hid, semM.at[0]).start()
    for t in range(DEPTH_A):
        issueA(jnp.int32(t))
    for b in range(DEPTH_B):
        issueB(jnp.int32(b))
    for c in range(2):
        kv_copy(jnp.int32(c)).start()
    copy(kpe, kp, semM.at[1]).start()
    copy(router, wR, semM.at[2]).start()

    barrier = pltpu.get_barrier_semaphore()
    for k in range(1, 8):
        pl.semaphore_signal(barrier, inc=1, device_id=(dp, lax.rem(me + k, 8)), device_id_type=MESH)

    row_id = lax.broadcasted_iota(jnp.int32, (tokens, ROPE_DIM), 0)
    posv = jnp.zeros((tokens, ROPE_DIM), jnp.int32)
    for t in range(tokens):
        posv = jnp.where(row_id == t, pos_ref[t], posv)
    angle = posv.astype(F4) * freq_ref[0:1, 0:ROPE_DIM]
    cosine = jnp.cos(angle)
    sine = jnp.sin(angle) * freq_ref[1:2, 0:ROPE_DIM]

    def rotate(v):
        other = jnp.concatenate([v[:, ROPE_DIM // 2:], v[:, :ROPE_DIM // 2]], axis=1)
        return v * cosine + other * sine

    def gain(ref):
        return ref[...].astype(F4).reshape(1, -1)

    def rms(v, gain):
        scale = lax.rsqrt(jnp.mean(v * v, axis=-1, keepdims=True) + EPSILON)
        return v * scale * gain

    copy(hidden, hid, semM.at[0]).wait()
    own = rows(chip)
    U[own, :] = rms(hid[...].astype(F4), gain(ag_ref)).astype(BF)

    def dq_step(t, carry):
        wait_whole(t)
        cq[:, cols(t, COL_TILE)] = dot(U[own, :], wA[lax.rem(t, DEPTH_A)])
        issueA(t + DEPTH_A)
        return carry

    lax.fori_loop(0, n_dq, dq_step, 0)
    kvs[...] = jnp.zeros_like(kvs)
    c_q = rms(cq[...], gain(qg_ref)).astype(BF)
    cq[...] = c_q.astype(F4)

    def put(ref, h, val):
        for g in range(tokens // SUB):
            ref[g, h] = val[g * SUB:(g + 1) * SUB]

    def uq_step(b, carry):
        slot = lax.rem(b, DEPTH_B)
        copy(uq.at[:, 0:Q_TILE], wB.at[slot, 0:q_rank, 0:Q_TILE], semB.at[slot]).wait()
        q2 = dot(cq[...].astype(BF), wB[slot, 0:q_rank, 0:Q_TILE]).astype(BF).astype(F4)
        issueB(b + DEPTH_B)
        for i in range(2):
            base = i * QK_DIM
            QN[2 * b + i] = q2[:, base:base + NOPE_DIM].astype(BF)
            put(QR, 2 * b + i, rotate(q2[:, base + NOPE_DIM:base + QK_DIM]).astype(BF).astype(F4))

        @pl.when(b < n_kv)
        def _():
            kv_copy(b).wait()
            kvs[...] = kvs[...] + dot_t(U[own, cols(b, KV_ROWS)], wD[lax.rem(b, 2)])

            @pl.when(b + 2 < n_kv)
            def _():
                kv_copy(b + 2).start()
        return carry

    lax.fori_loop(0, n_q, uq_step, 0)

    cnew_ref[...] = rms(kvs[:, 0:rank], gain(kg_ref)).astype(BF)
    knew_ref[...] = rotate(kvs[:, rank:rank + ROPE_DIM]).astype(BF)

    waitB(B_UK)
    slot_uk = B_UK % DEPTH_B

    for h in range(HEADS):
        w_h = wB[slot_uk, (h // 4) * rank:(h // 4 + 1) * rank, (h % 4) * NOPE_DIM:(h % 4 + 1) * NOPE_DIM]
        put(QA, h, dot_t(QN[h], w_h).astype(BF).astype(F4))
    issueB(jnp.int32(B_UK + DEPTH_B))

    waitB(B_CKV)
    slot_ckv = B_CKV % DEPTH_B
    copy(kpe, kp, semM.at[1]).wait()
    span = SUB * CACHE
    scale = QK_DIM ** -0.5
    lane = lax.broadcasted_iota(jnp.int32, (SUB, span), 1)
    tok = lax.broadcasted_iota(jnp.int32, (SUB, span), 0)
    for g in range(tokens // SUB):
        keys = wB[slot_ckv, g * span:(g + 1) * span, :]
        qa = QA[g]
        qr = QR[g]
        cn = cnew_ref[g * SUB:(g + 1) * SUB, :].astype(F4)
        kn = knew_ref[g * SUB:(g + 1) * SUB, :].astype(F4)
        s = dot_t(qa.reshape(HEADS * SUB, rank).astype(BF), keys)
        s = s + dot_t(qr.reshape(HEADS * SUB, ROPE_DIM).astype(BF), kp[g * span:(g + 1) * span, :])
        s = s.reshape(HEADS, SUB, span) * scale
        limit = posv[g * SUB:(g + 1) * SUB, 0:1]
        valid = (lane >= tok * CACHE) & (lane < tok * CACHE + limit)
        s = jnp.where(valid[None], s, -1e30)
        s_self = (jnp.sum(qa * cn[None], axis=2, keepdims=True) + jnp.sum(qr * kn[None], axis=2, keepdims=True)) * scale
        peak = jnp.maximum(jnp.max(s, axis=2, keepdims=True), s_self)
        e = jnp.where(valid[None], jnp.exp(s - peak), 0.0)
        e_self = jnp.exp(s_self - peak)
        denom = jnp.sum(e, axis=2, keepdims=True) + e_self
        p = (e / denom).astype(BF)
        p_self = (e_self / denom).astype(BF).astype(F4)
        ctx = dot(p.reshape(HEADS * SUB, span), keys).reshape(HEADS, SUB, rank) + p_self * cn[None]
        CTX[g] = ctx.astype(BF).astype(F4)
    issueB(jnp.int32(B_CKV + DEPTH_B))

    waitB(B_UV)
    slot_uv = B_UV % DEPTH_B
    for h in range(HEADS):
        w_h = wB[slot_uv, (h // 4) * rank:(h // 4 + 1) * rank, (h % 4) * VALUE_DIM:(h % 4 + 1) * VALUE_DIM]
        O[:, h * VALUE_DIM:(h + 1) * VALUE_DIM] = dot(CTX[:, h].reshape(tokens, rank).astype(BF), w_h).astype(BF)
    issueB(jnp.int32(B_UV + DEPTH_B))

    pl.semaphore_wait(barrier, 7)

    def grp_x(p, block):
        return rcopy(xm.at[:, cols(p, GROUP)], U.at[rows(block), cols(p, GROUP)], px_s.at[p], px_r.at[p], X)

    def grp_y(p, block):
        return rcopy(xm.at[:, cols(p, GROUP)], U.at[rows(block), cols(p, GROUP)], py_s.at[p], py_r.at[p], Y)

    def pass_y(p, block):
        return rcopy(U.at[rows(kX), cols(p, GROUP)], U.at[rows(block), cols(p, GROUP)], pr_s.at[p], pr_r.at[p], Y)

    def pass_x(p, block):
        return rcopy(U.at[rows(kY), cols(p, GROUP)], U.at[rows(block), cols(p, GROUP)], pr_s.at[p], pr_r.at[p], X)

    def forward(p):
        grp_x(p, kX).wait_recv()
        grp_y(p, kY).wait_recv()
        odd = lax.rem(p, 2)

        @pl.when(odd == 0)
        def _():
            pass_y(p, kX).start()

        @pl.when(odd == 1)
        def _():
            pass_x(p, kY).start()

    def out_step(j, carry):
        b = B_O + j
        waitB(b)
        att = dot(O[...], wB[lax.rem(b, DEPTH_B)])
        xm[:, cols(j, COL_TILE)] = (hid[:, cols(j, COL_TILE)].astype(F4) + att).astype(BF)
        issueB(b + DEPTH_B)

        @pl.when(lax.rem(j, 2) == 1)
        def _():
            p = j // 2
            grp_x(p, chip).start()
            grp_y(p, chip).start()

            @pl.when(p >= 3)
            def _():
                forward(p - 3)
        return carry

    lax.fori_loop(0, n_col, out_step, 0)
    toS = rcopy(xm, U.at[rows(4 + chip), :], d_s.at[0], d_r.at[0], sib)
    toS.start()

    xf = xm[...].astype(F4)
    row_scale = lax.rsqrt(jnp.mean(xf * xf, axis=-1, keepdims=True) + EPSILON)
    u_own = (xf * row_scale * gain(fg_ref)).astype(BF)
    U[own, :] = u_own
    copy(router, wR, semM.at[2]).wait()
    experts = router.shape[0]
    capacity = (CAP_FACTOR * tokens * topk_ref.shape[0] + experts - 1) // experts
    gates = jax.nn.sigmoid(dot_t(U[own, :], wR[...]))
    eid = lax.broadcasted_iota(jnp.int32, (experts, tokens), 0)
    picks = jnp.zeros((experts, tokens), F4)
    for k in range(topk_ref.shape[0]):
        picks = picks + jnp.where(topk_ref[k:k + 1, :] == eid, 1.0, 0.0)
    picks = picks.astype(BF)
    here = lax.broadcasted_iota(jnp.int32, (tokens, tokens), 0)
    there = lax.broadcasted_iota(jnp.int32, (tokens, tokens), 1)
    hits = dot_t(jnp.where(here == there, 1.0, 0.0).astype(BF), picks)
    before = dot_t(jnp.where(here > there, 1.0, 0.0).astype(BF), picks)
    total = jnp.sum(hits * gates, axis=1, keepdims=True)
    table = jnp.where(before < capacity, hits, 0.0) * (ROUTE_SCALE * gates / total)
    WT[own, 0:experts] = table
    WT[own, SCALE_LANE:LANES] = jnp.broadcast_to(row_scale, (tokens, LANES - SCALE_LANE))

    def table_to(k):
        dev = lax.rem(me + k, 8)
        block = chip + 4 * lax.rem(core + dev, 2)
        return rcopy(WT.at[own, :], WT.at[rows(block), :], w_s.at[k], w_r.at[k], dev)

    def table_from(k):
        dev = lax.rem(me + 8 - k, 8)
        block = dev // 2 + 4 * lax.rem(core + dev, 2)
        return rcopy(WT.at[rows(block), :], WT.at[rows(block), :], w_s.at[k], w_r.at[k], dev)

    for k in range(1, 8):
        table_to(k).start()

    def gated(both):
        g = both[:, 0:FF_TILE]
        return (g * jax.nn.sigmoid(g) * both[:, FF_TILE:2 * FF_TILE]).astype(BF)

    def to_twin(i, k):
        return rcopy(U.at[rows(k), :], U.at[rows(4 + k), :], d_s.at[i], d_r.at[i], sib)

    def shared_early(n, carry):
        t = A_S0 + n
        wait_pair(t)
        acts[:, cols(n, FF_TILE)] = gated(dot(U[own, :], wA[lax.rem(t, DEPTH_A)]))
        issueA(t + DEPTH_A)

        @pl.when(n < 3)
        def _():
            forward(n_grp - 3 + n)

        @pl.when(n == 3)
        def _():
            to_twin(1, kX).start()
            to_twin(2, kY).start()
        return carry

    lax.fori_loop(0, EARLY, shared_early, 0)

    for p in range(n_grp):
        if p % 2 == 0:
            pass_y(p, kD).wait_recv()
        else:
            pass_x(p, kD).wait_recv()
    to_twin(3, kD).start()
    rcopy(xm, U.at[rows(4 + chip), :], d_s.at[0], d_r.at[0], sib).wait_recv()
    for i, k in ((1, kX), (2, kY), (3, kD)):
        rcopy(U.at[rows(k), :], U.at[rows(4 + k), :], d_s.at[i], d_r.at[i], sib).wait_recv()
    toS.wait_send()
    for i, k in ((1, kX), (2, kY), (3, kD)):
        to_twin(i, k).wait_send()
    for p in range(n_grp):
        grp_x(p, chip).wait_send()
        grp_y(p, chip).wait_send()
        if p % 2 == 0:
            pass_y(p, kX).wait_send()
        else:
            pass_x(p, kY).wait_send()
    for k in range(1, 8):
        table_from(k).wait_recv()

    def normalise(i, carry):
        block = lax.rem(chip + i, 8)
        r = rows(block)
        U[r, :] = (U[r, :].astype(F4) * WT[r, SCALE_LANE:SCALE_LANE + 1] * gain(fg_ref)).astype(BF)
        return carry

    lax.fori_loop(1, 8, normalise, 0)

    def routed_up_step(i, carry):
        t = A_R + i
        wait_pair(t)
        both = dot(U[...], wA[lax.rem(t, DEPTH_A)])
        ACT[i // n_ff, :, cols(lax.rem(i, n_ff), FF_TILE)] = gated(both)
        issueA(t + DEPTH_A)
        return carry

    lax.fori_loop(0, 2 * n_ff, routed_up_step, 0)

    for k in range(1, 8):
        table_to(k).wait_send()

    lane_id = lax.broadcasted_iota(jnp.int32, WT.shape, 1)
    w0 = jnp.sum(jnp.where(lane_id == 2 * me, WT[...], 0.0), axis=1, keepdims=True)
    w1 = jnp.sum(jnp.where(lane_id == 2 * me + 1, WT[...], 0.0), axis=1, keepdims=True)

    def to_sib(j):
        return rcopy(Ps.at[lax.rem(j, SIB_SLOTS)], R1.at[:, :, cols(j, COL_TILE)], sib_s.at[j], sib_r.at[j], sib)

    def first_leg(j, dev):
        return rcopy(Pm.at[kD, :, cols(j, COL_TILE)], RL.at[:, cols(j, COL_TILE)], rl_s.at[j], rl_r.at[j], dev)

    def last_x(j):
        return rcopy(Pm.at[kX, :, cols(j, COL_TILE)], RX.at[:, cols(j, COL_TILE)], x_s.at[j], x_r.at[j], X)

    def last_y(j):
        return rcopy(Pm.at[kY, :, cols(j, COL_TILE)], RY.at[:, cols(j, COL_TILE)], y_s.at[j], y_r.at[j], Y)

    def chip_sum(j):
        to_sib(j).wait_recv()
        Pm[:, :, cols(j, COL_TILE)] = Pm[:, :, cols(j, COL_TILE)] + R1[:, :, cols(j, COL_TILE)]
        odd = lax.rem(j, 2)

        @pl.when(odd == 0)
        def _():
            first_leg(j, X).start()
            last_x(j).start()

        @pl.when(odd == 1)
        def _():
            first_leg(j, Y).start()
            last_y(j).start()

    def relay(j):
        odd = lax.rem(j, 2)

        @pl.when(odd == 0)
        def _():
            first_leg(j, X).wait_recv()
            Pm[kY, :, cols(j, COL_TILE)] = Pm[kY, :, cols(j, COL_TILE)] + RL[:, cols(j, COL_TILE)]
            last_y(j).start()

        @pl.when(odd == 1)
        def _():
            first_leg(j, Y).wait_recv()
            Pm[kX, :, cols(j, COL_TILE)] = Pm[kX, :, cols(j, COL_TILE)] + RL[:, cols(j, COL_TILE)]
            last_x(j).start()

    def down_step(j, carry):
        b = B_D + 2 * j
        waitB(b)
        waitB(b + 1)
        e0 = dot(ACT[0], wB[lax.rem(b, DEPTH_B)]).astype(BF)
        e1 = dot(ACT[1], wB[lax.rem(b + 1, DEPTH_B)]).astype(BF)

        @pl.when(j >= SIB_SLOTS)
        def _():
            to_sib(j - SIB_SLOTS).wait_send()

        part = w0 * e0.astype(F4) + w1 * e1.astype(F4)
        Pm[:, :, cols(j, COL_TILE)] = part[0:4 * tokens].reshape(4, tokens, COL_TILE)
        Ps[lax.rem(j, SIB_SLOTS)] = part[4 * tokens:8 * tokens].reshape(4, tokens, COL_TILE)
        to_sib(j).start()
        issueB(b + DEPTH_B)
        issueB(b + 1 + DEPTH_B)

        @pl.when(j >= SIB_LAG)
        def _():
            chip_sum(j - SIB_LAG)

        @pl.when((j >= 5) & (lax.rem(j, 2) == 1))
        def _():
            relay((j - 5) // 2)
        return carry

    lax.fori_loop(0, n_col, down_step, 0)
    for j in range(n_col - SIB_LAG, n_col):
        chip_sum(jnp.int32(j))
    relayed = (n_col - 4) // 2

    def shared_late(i, carry):
        t = A_S1 + i
        wait_pair(t)
        acts[:, cols(EARLY + i, FF_TILE)] = gated(dot(U[own, :], wA[lax.rem(t, DEPTH_A)]))
        relay(relayed + i)
        return carry

    lax.fori_loop(0, n_ff - EARLY, shared_late, 0)
    relayed = relayed + n_ff - EARLY

    def shared_down_step(j, carry):
        b = B_S + j
        waitB(b)
        out_ref[:, cols(j, COL_TILE)] = dot(acts[...], wB[lax.rem(b, DEPTH_B)]).astype(BF)
        issueB(b + DEPTH_B)

        @pl.when((lax.rem(j, 2) == 1) & (relayed + j // 2 < n_col))
        def _():
            relay(relayed + j // 2)
        return carry

    lax.fori_loop(0, n_col, shared_down_step, 0)
    for j in range(relayed + n_col // 2, n_col):
        relay(jnp.int32(j))

    def finish(j, carry):
        last_x(j).wait_recv()
        last_y(j).wait_recv()
        s = cols(j, COL_TILE)
        routed = Pm[chip, :, s] + RX[:, s] + RY[:, s]
        out_ref[:, s] = (xm[:, s].astype(F4) + routed + out_ref[:, s].astype(F4)).astype(BF)

        @pl.when(j >= n_col - SIB_SLOTS)
        def _():
            to_sib(j).wait_send()

        first_leg(j, X).wait_send()
        last_x(j).wait_send()
        last_y(j).wait_send()
        return carry

    lax.fori_loop(0, n_col, finish, 0)


def layer_call(positions, topk_ids, gains, big):
    hidden, w_dq, w_uq = big[0], big[3], big[4]
    tokens, width = hidden.shape
    q_rank = w_dq.shape[1]
    rank = big[1].shape[1]
    ff = big[10].shape[1]
    total = 8 * tokens
    n_col = width // COL_TILE
    n_grp = width // GROUP
    half = ROPE_DIM // 2
    freq = np.zeros((8, LANES), np.float32)
    freq[0, :ROPE_DIM] = np.tile((ROPE_BASE ** (-np.arange(half) / half)).astype(np.float32), 2)
    freq[1, :ROPE_DIM] = np.repeat([-1.0, 1.0], half)
    vmem = pl.BlockSpec(memory_space=pltpu.VMEM)
    smem = pl.BlockSpec(memory_space=pltpu.SMEM)
    hbm = pl.BlockSpec(memory_space=pl.ANY)
    dma = pltpu.SemaphoreType.DMA
    return pl.pallas_call(
        layer_kernel,
        out_shape=(jax.ShapeDtypeStruct((tokens, width), BF), jax.ShapeDtypeStruct((tokens, rank), BF),
                   jax.ShapeDtypeStruct((tokens, ROPE_DIM), BF)),
        in_specs=[smem] + [vmem] * 6 + [hbm] * len(big),
        out_specs=(vmem, vmem, vmem),
        scratch_shapes=[
            pltpu.VMEM((total, width), BF),
            pltpu.VMEM((total, LANES), F4),
            pltpu.VMEM((DEPTH_A, width, 2 * FF_TILE), BF),
            pltpu.VMEM((DEPTH_B, ff, COL_TILE), BF),
            pltpu.VMEM((2, big[5].shape[0], KV_ROWS), BF),
            pltpu.VMEM(big[9].shape, BF),
            pltpu.VMEM(big[2].shape, BF),
            pltpu.VMEM((tokens, big[5].shape[0]), F4),
            pltpu.VMEM((tokens, width), BF),
            pltpu.VMEM((tokens, width), BF),
            pltpu.VMEM((tokens, q_rank), F4),
            pltpu.VMEM((HEADS, tokens, NOPE_DIM), BF),
            pltpu.VMEM((tokens // SUB, HEADS, SUB, rank), F4),
            pltpu.VMEM((tokens // SUB, HEADS, SUB, ROPE_DIM), F4),
            pltpu.VMEM((tokens // SUB, HEADS, SUB, rank), F4),
            pltpu.VMEM((tokens, HEADS * VALUE_DIM), BF),
            pltpu.VMEM((tokens, ff), BF),
            pltpu.VMEM((2, total, ff), BF),
            pltpu.VMEM((4, tokens, width), F4),
            pltpu.VMEM((SIB_SLOTS, 4, tokens, COL_TILE), F4),
            pltpu.VMEM((4, tokens, width), F4),
            pltpu.VMEM((tokens, width), F4),
            pltpu.VMEM((tokens, width), F4),
            pltpu.VMEM((tokens, width), F4),
            dma((2, DEPTH_A)), dma((DEPTH_B,)), dma((2,)), dma((3,)),
        ] + [dma((n_grp,))] * 6 + [dma((4,))] * 2 + [dma((8,))] * 2 + [dma((n_col,))] * 8,
        compiler_params=pltpu.CompilerParams(collective_id=0, has_side_effects=True, vmem_limit_bytes=67043328),
        name='decode_layer',
    )(positions, topk_ids, jnp.asarray(freq), *gains, *big)


def solution(mesh):
    batch = P(('dp', 'ep'))
    whole = P()
    by_expert = P('ep')

    def local_step(hidden, positions, ckv_cache, kpe_cache, topk_ids, attn_gain, w_dq, q_gain, w_uq, w_dkv, kv_gain, w_uk, w_uv, w_out, ffn_gain, w_router, w_gate, w_up, w_down, shared_gate, shared_up, shared_down):
        gains = [attn_gain, q_gain, kv_gain, ffn_gain]
        ckv = ckv_cache.reshape(-1, ckv_cache.shape[2])
        kpe = kpe_cache.reshape(-1, kpe_cache.shape[2])
        big = (hidden, ckv, kpe, w_dq, w_uq, w_dkv.T, w_uk, w_uv, w_out, w_router.T, shared_gate, shared_up, shared_down, w_gate, w_up, w_down)
        return layer_call(positions, topk_ids.T, gains, big)

    in_specs = (batch,) * 5 + (whole,) * 11 + (by_expert,) * 3 + (whole,) * 3
    return jax.shard_map(local_step, mesh=mesh, in_specs=in_specs, out_specs=(batch, batch, batch), check_vma=False)
```

time: 357 us -> 132 us (0.37); the launches traced: 352 us -> 131 us
  matrix products: 152 us -> 0 us
  Pallas kernels: 0 us -> 126 us
  blocking collectives: 95.8 us -> 0 us
  waiting for transfers between devices: 66.8 us -> 0 us
  local copies, waits for them, and re-layouts: 22.2 us -> 4.48 us
  other arithmetic: 10.5 us -> 0 us
  starting transfers between devices: 3.71 us -> 0 us
    dot_general x18 -> x0, matrix products: 152 us -> none  [the longest x1 28.3 us: expert_block(): jnp.einsum('slcf,lfd->slcd', act, w_down, preferred_element_type=jnp.floa...]
    pallas_call x0 -> x1, Pallas kernels: none -> 126 us  [layer_call(): pl.pallas_call(layer_kernel, out_shape=(jax.ShapeDtypeStruct((tokens, wid...]
    all_to_all x1 -> x0, blocking collectives: 95.8 us -> none  [local_step(): lax.all_to_all(outgoing, 'ep', 0, 0, tiled=True)]
    all_to_all x1 -> x0, waiting for transfers between devices: 66.8 us -> none  [local_step(): returned = lax.all_to_all(results, 'ep', 0, 0, tiled=True)]
    gather x6 -> x0, local copies, waits for them, and re-layouts: 14.5 us -> none  [the longest x1 12.1 us: local_step(): picked = jnp.take(returned, jnp.maximum(slots, 0), axis=0)]
    reduce_sum x7 -> x0, other arithmetic: 7.96 us -> none  [the longest x1 6.16 us: local_step(): routed = jnp.sum(weights[:, :, None] * picked.astype(jnp.float32), axis=1)]
    convert_element_type x1 -> x0, local copies, waits for them, and re-layouts: 6.76 us -> none  [expert_block(): jnp.einsum('slcf,lfd->slcd', act, w_down, preferred_element_type=jnp.floa...]
    unnamed x32 -> x3, local copies, waits for them, and re-layouts: 0.12 us -> 4.48 us
  transfers between devices with their start and end apart: 1 -> 0, of which waited for: 1 -> 0; matrix products, arithmetic and copies ran while one was open for 5% -> 0% of each run, Pallas kernels for 0% -> 0%
where the time goes in v2:
time: 132 us; the launch traced here: 131 us
  Pallas kernels  126 us (95%)
  local copies, waits for them, and re-layouts  4.48 us (3%)
    pallas_call x1, Pallas kernels, layer_call(): pl.pallas_call(layer_kernel, out_shape=(jax.ShapeDtypeStruct((tokens, wid...  126 us
    unnamed x3, local copies, waits for them, and re-layouts  4.48 us

profile of v2, /device:TPU:0, one launch (start us, length us, event | category | flops | bytes accessed | tf_op | source)
XLA Modules:
  0.0 131.3 jit_solution(11858005609951425181)
XLA Ops:
  0.6 126.1 %decode_layer.1 = (bf16[32,7168]{1,0:T(8,128)(2,1)}, bf16[32,512]{1,0:T(8,128)(2,1)}, bf16[32,64]{1,0:T(8,128)(2,1)}) custom-call(s32[32]{0:T(128)} %pos_ref.1, s32[8,32]{1,0:T(8,128)} %bitcast.9, f32[8,128]{1,0:T(8,128)} %constant.2.clone.freq_ref, bf16[7168]{0:T(1024)(128)(2,1)} %ag_ref.1, bf16[1536]{0:T(1024)(128)(2,1)} %qg_ref.1, bf16[512]{0:T(512)(128)(2,1)} %kg_ref.1, ...), custom_call_target="tpu_custom_call" | custom-call | tf_op jit(solution)/shard_map/decode_layer/pallas_call | solution.py:591
  126.8 1.8 %copy.29 = bf16[32,7168]{1,0:T(8,128)(2,1)} copy(bf16[32,7168]{1,0:T(8,128)(2,1)} %get-tuple-element.6) | data formatting | bytes 917504
  128.6 1.4 %copy.30 = bf16[32,512]{1,0:T(8,128)(2,1)} copy(bf16[32,512]{1,0:T(8,128)(2,1)} %get-tuple-element.7) | data formatting | bytes 65536
  130.0 1.3 copy.31

commit v3 on v2

--- a/solution.py
+++ b/solution.py
@@ -20,25 +20,28 @@
 FF_TILE = 256
 COL_TILE = 512
 Q_TILE = 2 * QK_DIM
-GROUP = 1024
-KV_ROWS = 1024
+GROUP = 512
+PASS_LAG = 3
+KV_TILES = 3
+RELAY_LAG = 4
+A_AT = 4
+DONE_LAG = 6
 DEPTH_A = 3
-DEPTH_B = 7
+DEPTH_B = 8
 LANES = 128
-SCALE_LANE = 64
-SIB_LAG = 2
+SIB_LAG = 1
 SIB_SLOTS = 4
-EARLY = 5
 SUB = 8
 BF = jnp.bfloat16
 F4 = jnp.float32
 
 
-def layer_kernel(pos_ref, topk_ref, freq_ref, ag_ref, qg_ref, kg_ref, fg_ref,
+def layer_kernel(pos_ref, topk, freq, ag, qg, kg, fg,
                  hidden, ckv, kpe, dq, uq, dkv, uk, uv, wo, router, sg, su, sd, wg, wu, wd,
-                 out_ref, cnew_ref, knew_ref,
-                 U, WT, wA, wB, wD, wR, kp, kvs, hid, xm, cq, QN, QA, QR, CTX, O, acts, ACT, Pm, Ps, R1, RL, RX, RY,
-                 semA, semB, semD, semM, px_s, px_r, py_s, py_r, pr_s, pr_r, d_s, d_r, w_s, w_r,
+                 out_hbm, cnew_hbm, knew_hbm,
+                 topk_ref, freq_ref, ag_ref, qg_ref, kg_ref, fg_ref, out_ref, cnew_ref, knew_ref,
+                 U, WT, wA, wB, wR, kp, kvs, hid, xm, cq, QN, QA, QR, CTX, O, acts, part_s, H, ACT, Pm, Ps, R1, RL, RX, RY,
+                 semA, semB, semM, as_s, as_r, px_s, px_r, py_s, py_r, pr_s, pr_r, d_s, d_r, w_s, w_r,
                  sib_s, sib_r, rl_s, rl_r, x_s, x_r, y_s, y_r):
     tokens, width = hid.shape
     ff = sg.shape[1]
@@ -49,6 +52,8 @@
     n_grp = width // GROUP
     n_q = uq.shape[1] // Q_TILE
     n_dq = q_rank // COL_TILE
+    kv_dim = dkv.shape[0]
+    n_kv = (width // COL_TILE + KV_TILES - 1) // KV_TILES
     dp = lax.axis_index('dp')
     me = lax.axis_index('ep')
     core = lax.rem(me, 2)
@@ -82,9 +87,8 @@
         return lax.dot_general(a, b, (((1,), (1,)), ((), ())), preferred_element_type=F4)
 
     A_S0 = n_dq
-    A_R = A_S0 + EARLY
-    A_S1 = A_R + 2 * n_ff
-    A_END = A_S1 + n_ff - EARLY
+    A_R = A_S0 + 1
+    A_END = A_R + 2 * n_ff
 
     def issueA(t):
         slot = lax.rem(t, DEPTH_A)
@@ -97,21 +101,15 @@
         def _():
             copy(dq.at[:, cols(t, COL_TILE)], wA.at[slot], semA.at[0, slot]).start()
 
-        @pl.when((t >= A_S0) & (t < A_R))
-        def _():
-            n = t - A_S0
-            pair(sg.at[:, cols(n, FF_TILE)], su.at[:, cols(n, FF_TILE)])
-
-        @pl.when((t >= A_R) & (t < A_S1))
+        @pl.when(t == A_S0)
+        def _():
+            pair(sg.at[:, cols(me, FF_TILE)], su.at[:, cols(me, FF_TILE)])
+
+        @pl.when((t >= A_R) & (t < A_END))
         def _():
             e = (t - A_R) // n_ff
             n = lax.rem(t - A_R, n_ff)
             pair(wg.at[e, :, cols(n, FF_TILE)], wu.at[e, :, cols(n, FF_TILE)])
-
-        @pl.when((t >= A_S1) & (t < A_END))
-        def _():
-            n = t - A_S1 + EARLY
-            pair(sg.at[:, cols(n, FF_TILE)], su.at[:, cols(n, FF_TILE)])
 
     def wait_whole(t):
         slot = lax.rem(t, DEPTH_A)
@@ -122,10 +120,11 @@
         copy(sg.at[:, 0:FF_TILE], wA.at[slot, :, 0:FF_TILE], semA.at[0, slot]).wait()
         copy(su.at[:, 0:FF_TILE], wA.at[slot, :, FF_TILE:2 * FF_TILE], semA.at[1, slot]).wait()
 
-    B_UK = n_q
-    B_CKV = n_q + 1
-    B_UV = n_q + 2
-    B_O = n_q + 3
+    B_Q = n_kv
+    B_UK = B_Q + n_q
+    B_CKV = B_UK + 1
+    B_UV = B_UK + 2
+    B_O = B_UK + 3
     B_D = B_O + n_col
     B_S = B_D + 2 * n_col
     B_END = B_S + n_col
@@ -137,9 +136,9 @@
             for q in range(4):
                 copy(src.at[:, q * COL_TILE:(q + 1) * COL_TILE], wB.at[slot, q * rank:(q + 1) * rank, :], semB.at[slot]).start()
 
-        @pl.when(b < n_q)
-        def _():
-            copy(uq.at[:, cols(b, Q_TILE)], wB.at[slot, 0:q_rank, 0:Q_TILE], semB.at[slot]).start()
+        @pl.when((b >= B_Q) & (b < B_UK))
+        def _():
+            copy(uq.at[:, cols(b - B_Q, Q_TILE)], wB.at[slot, 0:q_rank, 0:Q_TILE], semB.at[slot]).start()
 
         @pl.when(b == B_UK)
         def _():
@@ -169,25 +168,68 @@
         slot = lax.rem(b, DEPTH_B)
         copy(sd.at[:, 0:COL_TILE], wB.at[slot], semB.at[slot]).wait()
 
-    n_kv = width // KV_ROWS
-
-    def kv_copy(c):
-        slot = lax.rem(c, 2)
-        return copy(dkv.at[:, cols(c, KV_ROWS)], wD.at[slot], semD.at[slot])
-
-    copy(hidden, hid, semM.at[0]).start()
-    for t in range(DEPTH_A):
-        issueA(jnp.int32(t))
-    for b in range(DEPTH_B):
-        issueB(jnp.int32(b))
-    for c in range(2):
-        kv_copy(jnp.int32(c)).start()
-    copy(kpe, kp, semM.at[1]).start()
-    copy(router, wR, semM.at[2]).start()
+    def kv_tiles(b):
+        return min(KV_TILES, n_col - b * KV_TILES)
+
+    def issue_kv(b):
+        for i in range(kv_tiles(b)):
+            first = (b * KV_TILES + i) * COL_TILE
+            copy(dkv.at[:, first:first + COL_TILE], wB.at[b, i * kv_dim:(i + 1) * kv_dim, :], semB.at[b]).start()
+
+    def wait_kv(b):
+        span = kv_tiles(b) * kv_dim
+        copy(sd.at[0:span, 0:COL_TILE], wB.at[b, 0:span, :], semB.at[b]).wait()
+
+    small = [copy(hidden, hid, semM.at[0]), copy(kpe, kp, semM.at[1]), copy(router, wR, semM.at[2]), copy(topk, topk_ref, semM.at[3]),
+             copy(freq, freq_ref, semM.at[4]), copy(ag, ag_ref, semM.at[5]), copy(qg, qg_ref, semM.at[6]), copy(kg, kg_ref, semM.at[7]), copy(fg, fg_ref, semM.at[8])]
+    small[0].start()
+    small[5].start()
+    small[4].start()
+    for b in range(n_kv):
+        issue_kv(b)
+    issueA(jnp.int32(0))
+    issueA(jnp.int32(1))
+    for i in (6, 7, 8, 3, 1, 2):
+        small[i].start()
 
     barrier = pltpu.get_barrier_semaphore()
     for k in range(1, 8):
         pl.semaphore_signal(barrier, inc=1, device_id=(dp, lax.rem(me + k, 8)), device_id_type=MESH)
+
+    def rotate(v):
+        other = jnp.concatenate([v[:, ROPE_DIM // 2:], v[:, :ROPE_DIM // 2]], axis=1)
+        return v * cosine + other * sine
+
+    def gain(ref):
+        return ref[...].astype(F4).reshape(1, -1)
+
+    def rms(v, gain):
+        scale = lax.rsqrt(jnp.mean(v * v, axis=-1, keepdims=True) + EPSILON)
+        return v * scale * gain
+
+    small[0].wait()
+    small[5].wait()
+    own = rows(chip)
+    U[own, :] = rms(hid[...].astype(F4), gain(ag_ref)).astype(BF)
+
+    kvs[...] = jnp.zeros_like(kvs)
+    for b in range(n_kv):
+        wait_kv(b)
+        part = kvs[...]
+        for i in range(kv_tiles(b)):
+            first = (b * KV_TILES + i) * COL_TILE
+            part = part + dot_t(U[own, first:first + COL_TILE], wB[b, i * kv_dim:(i + 1) * kv_dim, :])
+        kvs[...] = part
+        if b == 0:
+            issueA(jnp.int32(2))
+    for b in range(n_kv, n_kv + DEPTH_B):
+        issueB(jnp.int32(b))
+    for t in range(n_dq):
+        wait_whole(t)
+        cq[:, t * COL_TILE:(t + 1) * COL_TILE] = dot(U[own, :], wA[t])
+    small[6].wait()
+    small[7].wait()
+    small[4].wait()
 
     row_id = lax.broadcasted_iota(jnp.int32, (tokens, ROPE_DIM), 0)
     posv = jnp.zeros((tokens, ROPE_DIM), jnp.int32)
@@ -196,30 +238,6 @@
     angle = posv.astype(F4) * freq_ref[0:1, 0:ROPE_DIM]
     cosine = jnp.cos(angle)
     sine = jnp.sin(angle) * freq_ref[1:2, 0:ROPE_DIM]
-
-    def rotate(v):
-        other = jnp.concatenate([v[:, ROPE_DIM // 2:], v[:, :ROPE_DIM // 2]], axis=1)
-        return v * cosine + other * sine
-
-    def gain(ref):
-        return ref[...].astype(F4).reshape(1, -1)
-
-    def rms(v, gain):
-        scale = lax.rsqrt(jnp.mean(v * v, axis=-1, keepdims=True) + EPSILON)
-        return v * scale * gain
-
-    copy(hidden, hid, semM.at[0]).wait()
-    own = rows(chip)
-    U[own, :] = rms(hid[...].astype(F4), gain(ag_ref)).astype(BF)
-
-    def dq_step(t, carry):
-        wait_whole(t)
-        cq[:, cols(t, COL_TILE)] = dot(U[own, :], wA[lax.rem(t, DEPTH_A)])
-        issueA(t + DEPTH_A)
-        return carry
-
-    lax.fori_loop(0, n_dq, dq_step, 0)
-    kvs[...] = jnp.zeros_like(kvs)
     c_q = rms(cq[...], gain(qg_ref)).astype(BF)
     cq[...] = c_q.astype(F4)
 
@@ -227,30 +245,33 @@
         for g in range(tokens // SUB):
             ref[g, h] = val[g * SUB:(g + 1) * SUB]
 
-    def uq_step(b, carry):
-        slot = lax.rem(b, DEPTH_B)
-        copy(uq.at[:, 0:Q_TILE], wB.at[slot, 0:q_rank, 0:Q_TILE], semB.at[slot]).wait()
-        q2 = dot(cq[...].astype(BF), wB[slot, 0:q_rank, 0:Q_TILE]).astype(BF).astype(F4)
-        issueB(b + DEPTH_B)
-        for i in range(2):
-            base = i * QK_DIM
-            QN[2 * b + i] = q2[:, base:base + NOPE_DIM].astype(BF)
-            put(QR, 2 * b + i, rotate(q2[:, base + NOPE_DIM:base + QK_DIM]).astype(BF).astype(F4))
-
-        @pl.when(b < n_kv)
-        def _():
-            kv_copy(b).wait()
-            kvs[...] = kvs[...] + dot_t(U[own, cols(b, KV_ROWS)], wD[lax.rem(b, 2)])
-
-            @pl.when(b + 2 < n_kv)
-            def _():
-                kv_copy(b + 2).start()
+    def uq_step(i, carry):
+        parts = []
+        for k in range(2):
+            b = B_Q + 2 * i + k
+            slot = lax.rem(b, DEPTH_B)
+            copy(uq.at[:, 0:Q_TILE], wB.at[slot, 0:q_rank, 0:Q_TILE], semB.at[slot]).wait()
+        for k in range(2):
+            b = B_Q + 2 * i + k
+            parts.append(dot(cq[...].astype(BF), wB[lax.rem(b, DEPTH_B), 0:q_rank, 0:Q_TILE]).astype(BF).astype(F4))
+        for k in range(2):
+            issueB(B_Q + 2 * i + k + DEPTH_B)
+        for h in range(4):
+            q2 = parts[h // 2]
+            base = (h % 2) * QK_DIM
+            QN[4 * i + h] = q2[:, base:base + NOPE_DIM].astype(BF)
+            put(QR, 4 * i + h, rotate(q2[:, base + NOPE_DIM:base + QK_DIM]).astype(BF).astype(F4))
         return carry
 
-    lax.fori_loop(0, n_q, uq_step, 0)
+    lax.fori_loop(0, n_q // 2, uq_step, 0)
+    issueA(jnp.int32(n_dq))
 
     cnew_ref[...] = rms(kvs[:, 0:rank], gain(kg_ref)).astype(BF)
     knew_ref[...] = rotate(kvs[:, rank:rank + ROPE_DIM]).astype(BF)
+    c_out = copy(cnew_ref, cnew_hbm, semM.at[9])
+    k_out = copy(knew_ref, knew_hbm, semM.at[10])
+    c_out.start()
+    k_out.start()
 
     waitB(B_UK)
     slot_uk = B_UK % DEPTH_B
@@ -262,7 +283,7 @@
 
     waitB(B_CKV)
     slot_ckv = B_CKV % DEPTH_B
-    copy(kpe, kp, semM.at[1]).wait()
+    small[1].wait()
     span = SUB * CACHE
     scale = QK_DIM ** -0.5
     lane = lax.broadcasted_iota(jnp.int32, (SUB, span), 1)
@@ -312,45 +333,63 @@
         return rcopy(U.at[rows(kY), cols(p, GROUP)], U.at[rows(block), cols(p, GROUP)], pr_s.at[p], pr_r.at[p], X)
 
     def forward(p):
-        grp_x(p, kX).wait_recv()
-        grp_y(p, kY).wait_recv()
         odd = lax.rem(p, 2)
 
         @pl.when(odd == 0)
         def _():
+            grp_x(p, kX).wait_recv()
             pass_y(p, kX).start()
 
         @pl.when(odd == 1)
         def _():
+            grp_y(p, kY).wait_recv()
             pass_x(p, kY).start()
 
-    def out_step(j, carry):
-        b = B_O + j
+    def send_rest(first, last):
+        for p in range(first, last):
+            if p % 2 == 0:
+                grp_y(p, chip).start()
+            else:
+                grp_x(p, chip).start()
+
+    def out_step(i, carry):
+        b = B_O + 2 * i
         waitB(b)
-        att = dot(O[...], wB[lax.rem(b, DEPTH_B)])
-        xm[:, cols(j, COL_TILE)] = (hid[:, cols(j, COL_TILE)].astype(F4) + att).astype(BF)
+        waitB(b + 1)
+        both = [dot(O[...], wB[lax.rem(b + k, DEPTH_B)]) for k in range(2)]
+        for k in range(2):
+            s = cols(2 * i + k, COL_TILE)
+            xm[:, s] = (hid[:, s].astype(F4) + both[k]).astype(BF)
+        grp_x(2 * i, chip).start()
+        grp_y(2 * i + 1, chip).start()
         issueB(b + DEPTH_B)
-
-        @pl.when(lax.rem(j, 2) == 1)
-        def _():
-            p = j // 2
-            grp_x(p, chip).start()
-            grp_y(p, chip).start()
-
-            @pl.when(p >= 3)
-            def _():
-                forward(p - 3)
+        issueB(b + 1 + DEPTH_B)
+
+        @pl.when(i < PASS_LAG)
+        def _():
+            grp_y(2 * i, chip).start()
+            grp_x(2 * i + 1, chip).start()
+
+        @pl.when(i >= PASS_LAG)
+        def _():
+            forward(2 * (i - PASS_LAG))
+            forward(2 * (i - PASS_LAG) + 1)
+
+        @pl.when((i >= A_AT) & (i < A_AT + DEPTH_A - 1))
+        def _():
+            issueA(i - A_AT + n_dq + 1)
         return carry
 
-    lax.fori_loop(0, n_col, out_step, 0)
-    toS = rcopy(xm, U.at[rows(4 + chip), :], d_s.at[0], d_r.at[0], sib)
+    lax.fori_loop(0, n_col // 2, out_step, 0)
+    send_rest(2 * PASS_LAG, 2 * PASS_LAG + 2)
+
+    small[8].wait()
+    u_own = rms(xm[...].astype(F4), gain(fg_ref)).astype(BF)
+    U[own, :] = u_own
+    toS = rcopy(U.at[own, :], U.at[rows(4 + chip), :], d_s.at[0], d_r.at[0], sib)
     toS.start()
-
-    xf = xm[...].astype(F4)
-    row_scale = lax.rsqrt(jnp.mean(xf * xf, axis=-1, keepdims=True) + EPSILON)
-    u_own = (xf * row_scale * gain(fg_ref)).astype(BF)
-    U[own, :] = u_own
-    copy(router, wR, semM.at[2]).wait()
+    small[2].wait()
+    small[3].wait()
     experts = router.shape[0]
     capacity = (CAP_FACTOR * tokens * topk_ref.shape[0] + experts - 1) // experts
     gates = jax.nn.sigmoid(dot_t(U[own, :], wR[...]))
@@ -366,20 +405,22 @@
     total = jnp.sum(hits * gates, axis=1, keepdims=True)
     table = jnp.where(before < capacity, hits, 0.0) * (ROUTE_SCALE * gates / total)
     WT[own, 0:experts] = table
-    WT[own, SCALE_LANE:LANES] = jnp.broadcast_to(row_scale, (tokens, LANES - SCALE_LANE))
-
-    def table_to(k):
-        dev = lax.rem(me + k, 8)
-        block = chip + 4 * lax.rem(core + dev, 2)
-        return rcopy(WT.at[own, :], WT.at[rows(block), :], w_s.at[k], w_r.at[k], dev)
-
-    def table_from(k):
-        dev = lax.rem(me + 8 - k, 8)
-        block = dev // 2 + 4 * lax.rem(core + dev, 2)
-        return rcopy(WT.at[rows(block), :], WT.at[rows(block), :], w_s.at[k], w_r.at[k], dev)
-
-    for k in range(1, 8):
-        table_to(k).start()
+
+    WT[own, experts:LANES] = jnp.zeros((tokens, LANES - experts), F4)
+    D = kD * 2 + core
+    mates = ((1, kX, X), (2, kY, Y), (3, kD, D))
+
+    def table_to(i, dev):
+        return rcopy(WT.at[own, :], WT.at[own, :], w_s.at[i], w_r.at[i], dev)
+
+    def table_from(i, k, dev):
+        return rcopy(WT.at[rows(k), :], WT.at[rows(k), :], w_s.at[i], w_r.at[i], dev)
+
+    def tables_to_twin():
+        return rcopy(WT.at[0:4 * tokens, :], WT.at[4 * tokens:8 * tokens, :], w_s.at[0], w_r.at[0], sib)
+
+    for i, _, dev in mates:
+        table_to(i, dev).start()
 
     def gated(both):
         g = both[:, 0:FF_TILE]
@@ -388,66 +429,83 @@
     def to_twin(i, k):
         return rcopy(U.at[rows(k), :], U.at[rows(4 + k), :], d_s.at[i], d_r.at[i], sib)
 
-    def shared_early(n, carry):
-        t = A_S0 + n
-        wait_pair(t)
-        acts[:, cols(n, FF_TILE)] = gated(dot(U[own, :], wA[lax.rem(t, DEPTH_A)]))
-        issueA(t + DEPTH_A)
-
-        @pl.when(n < 3)
-        def _():
-            forward(n_grp - 3 + n)
-
-        @pl.when(n == 3)
-        def _():
-            to_twin(1, kX).start()
-            to_twin(2, kY).start()
-        return carry
-
-    lax.fori_loop(0, EARLY, shared_early, 0)
-
+    def normalise(block):
+        r = rows(block)
+        U[r, :] = rms(U[r, :].astype(F4), gain(fg_ref)).astype(BF)
+
+    for p in range(n_grp - 2 * PASS_LAG, n_grp, 2):
+        forward(jnp.int32(p))
+        forward(jnp.int32(p + 1))
+        if p > n_grp - 2 * PASS_LAG:
+            q = p - n_grp + 4 * PASS_LAG
+            send_rest(min(q, n_grp), min(q + 2, n_grp))
+    send_rest(4 * PASS_LAG, n_grp)
+    for p in range(1, n_grp, 2):
+        grp_x(p, kX).wait_recv()
+        pass_x(p, kY).wait_send()
+    for p in range(0, n_grp, 2):
+        pass_y(p, kX).wait_send()
+    normalise(kX)
+    to_twin(1, kX).start()
+    for p in range(0, n_grp, 2):
+        grp_y(p, kY).wait_recv()
+    normalise(kY)
+    to_twin(2, kY).start()
     for p in range(n_grp):
         if p % 2 == 0:
             pass_y(p, kD).wait_recv()
         else:
             pass_x(p, kD).wait_recv()
+    normalise(kD)
     to_twin(3, kD).start()
-    rcopy(xm, U.at[rows(4 + chip), :], d_s.at[0], d_r.at[0], sib).wait_recv()
+    wait_pair(A_S0)
+    part_s[0:4 * tokens, :] = gated(dot(U[0:4 * tokens, :], wA[A_S0 % DEPTH_A]))
+    for i, k, dev in mates:
+        table_from(i, k, dev).wait_recv()
+    tables_to_twin().start()
+    rcopy(U.at[own, :], U.at[rows(4 + chip), :], d_s.at[0], d_r.at[0], sib).wait_recv()
     for i, k in ((1, kX), (2, kY), (3, kD)):
         rcopy(U.at[rows(k), :], U.at[rows(4 + k), :], d_s.at[i], d_r.at[i], sib).wait_recv()
+    part_s[4 * tokens:8 * tokens, :] = gated(dot(U[4 * tokens:8 * tokens, :], wA[A_S0 % DEPTH_A]))
+    issueA(jnp.int32(A_S0 + DEPTH_A))
     toS.wait_send()
     for i, k in ((1, kX), (2, kY), (3, kD)):
         to_twin(i, k).wait_send()
     for p in range(n_grp):
         grp_x(p, chip).wait_send()
         grp_y(p, chip).wait_send()
-        if p % 2 == 0:
-            pass_y(p, kX).wait_send()
-        else:
-            pass_x(p, kY).wait_send()
+
+    def act_to(k):
+        dev = lax.rem(me + k, 8)
+        block = dev // 2 + 4 * lax.rem(core + dev, 2)
+        return rcopy(part_s.at[rows(block), :], acts.at[:, cols(me, FF_TILE)], as_s.at[k], as_r.at[k], dev)
+
+    def act_from(k):
+        dev = lax.rem(me + 8 - k, 8)
+        return rcopy(part_s.at[own, :], acts.at[:, cols(dev, FF_TILE)], as_s.at[k], as_r.at[k], dev)
+
     for k in range(1, 8):
-        table_from(k).wait_recv()
-
-    def normalise(i, carry):
-        block = lax.rem(chip + i, 8)
-        r = rows(block)
-        U[r, :] = (U[r, :].astype(F4) * WT[r, SCALE_LANE:SCALE_LANE + 1] * gain(fg_ref)).astype(BF)
-        return carry
-
-    lax.fori_loop(1, 8, normalise, 0)
+        act_to(k).start()
+    acts[:, cols(me, FF_TILE)] = part_s[own, :]
 
     def routed_up_step(i, carry):
         t = A_R + i
         wait_pair(t)
-        both = dot(U[...], wA[lax.rem(t, DEPTH_A)])
-        ACT[i // n_ff, :, cols(lax.rem(i, n_ff), FF_TILE)] = gated(both)
+        last = i - 1
+        ACT[last // n_ff, :, cols(lax.rem(last, n_ff), FF_TILE)] = gated(H[lax.rem(last, 2)])
+        H[lax.rem(i, 2)] = dot(U[...], wA[lax.rem(t, DEPTH_A)])
         issueA(t + DEPTH_A)
         return carry
 
-    lax.fori_loop(0, 2 * n_ff, routed_up_step, 0)
-
-    for k in range(1, 8):
-        table_to(k).wait_send()
+    wait_pair(A_R)
+    H[0] = dot(U[...], wA[A_R % DEPTH_A])
+    issueA(jnp.int32(A_R + DEPTH_A))
+    lax.fori_loop(1, 2 * n_ff, routed_up_step, 0)
+    ACT[1, :, ff - FF_TILE:ff] = gated(H[(2 * n_ff - 1) % 2])
+
+    for i, _, dev in mates:
+        table_to(i, dev).wait_send()
+    tables_to_twin().wait()
 
     lane_id = lax.broadcasted_iota(jnp.int32, WT.shape, 1)
     w0 = jnp.sum(jnp.where(lane_id == 2 * me, WT[...], 0.0), axis=1, keepdims=True)
@@ -473,12 +531,18 @@
         @pl.when(odd == 0)
         def _():
             first_leg(j, X).start()
-            last_x(j).start()
+
+            @pl.when(j < RELAY_LAG)
+            def _():
+                last_x(j).start()
 
         @pl.when(odd == 1)
         def _():
             first_leg(j, Y).start()
-            last_y(j).start()
+
+            @pl.when(j < RELAY_LAG)
+            def _():
+                last_y(j).start()
 
     def relay(j):
         odd = lax.rem(j, 2)
@@ -517,40 +581,27 @@
         def _():
             chip_sum(j - SIB_LAG)
 
-        @pl.when((j >= 5) & (lax.rem(j, 2) == 1))
-        def _():
-            relay((j - 5) // 2)
+        @pl.when(j >= RELAY_LAG)
+        def _():
+            relay(j - RELAY_LAG)
         return carry
 
     lax.fori_loop(0, n_col, down_step, 0)
     for j in range(n_col - SIB_LAG, n_col):
         chip_sum(jnp.int32(j))
-    relayed = (n_col - 4) // 2
-
-    def shared_late(i, carry):
-        t = A_S1 + i
-        wait_pair(t)
-        acts[:, cols(EARLY + i, FF_TILE)] = gated(dot(U[own, :], wA[lax.rem(t, DEPTH_A)]))
-        relay(relayed + i)
-        return carry
-
-    lax.fori_loop(0, n_ff - EARLY, shared_late, 0)
-    relayed = relayed + n_ff - EARLY
-
-    def shared_down_step(j, carry):
-        b = B_S + j
-        waitB(b)
-        out_ref[:, cols(j, COL_TILE)] = dot(acts[...], wB[lax.rem(b, DEPTH_B)]).astype(BF)
-        issueB(b + DEPTH_B)
-
-        @pl.when((lax.rem(j, 2) == 1) & (relayed + j // 2 < n_col))
-        def _():
-            relay(relayed + j // 2)
-        return carry
-
-    lax.fori_loop(0, n_col, shared_down_step, 0)
-    for j in range(relayed + n_col // 2, n_col):
-        relay(jnp.int32(j))
+    for j in range(RELAY_LAG, n_col):
+        if j % 2 == 0:
+            last_x(jnp.int32(j)).start()
+        else:
+            last_y(jnp.int32(j)).start()
+    relayed = n_col - RELAY_LAG
+
+    for k in range(1, 8):
+        act_from(k).wait_recv()
+        act_to(k).wait_send()
+
+    def result(j):
+        return copy(out_ref.at[:, cols(j, COL_TILE)], out_hbm.at[:, cols(j, COL_TILE)], semM.at[11])
 
     def finish(j, carry):
         last_x(j).wait_recv()
@@ -558,17 +609,46 @@
         s = cols(j, COL_TILE)
         routed = Pm[chip, :, s] + RX[:, s] + RY[:, s]
         out_ref[:, s] = (xm[:, s].astype(F4) + routed + out_ref[:, s].astype(F4)).astype(BF)
-
-        @pl.when(j >= n_col - SIB_SLOTS)
-        def _():
+        result(j).start()
+        return carry
+
+    def shared_down_step(j, carry):
+        b = B_S + j
+        waitB(b)
+        out_ref[:, cols(j, COL_TILE)] = dot(acts[...], wB[lax.rem(b, DEPTH_B)]).astype(BF)
+        issueB(b + DEPTH_B)
+
+        @pl.when(relayed + j < n_col)
+        def _():
+            relay(relayed + j)
+
+        @pl.when(j >= DONE_LAG)
+        def _():
+            finish(j - DONE_LAG, 0)
+        return carry
+
+    lax.fori_loop(0, n_col, shared_down_step, 0)
+    lax.fori_loop(n_col - DONE_LAG, n_col, finish, 0)
+    for j in range(n_col):
+        if j >= n_col - SIB_SLOTS:
             to_sib(j).wait_send()
-
         first_leg(j, X).wait_send()
         last_x(j).wait_send()
         last_y(j).wait_send()
-        return carry
-
-    lax.fori_loop(0, n_col, finish, 0)
+    c_out.wait()
+    k_out.wait()
+    copy(out_ref, out_hbm, semM.at[11]).wait()
+
+
+def hand_on(a, b, c, oa, ob, oc, va, vb, vc, sems):
+    pairs = ((a, va, oa), (b, vb, ob), (c, vc, oc))
+    for i, (src, mid, _) in enumerate(pairs):
+        pltpu.make_async_copy(src, mid, sems.at[0, i]).start()
+    for i, (src, mid, dst) in enumerate(pairs):
+        pltpu.make_async_copy(src, mid, sems.at[0, i]).wait()
+        pltpu.make_async_copy(mid, dst, sems.at[1, i]).start()
+    for i, (_, mid, dst) in enumerate(pairs):
+        pltpu.make_async_copy(mid, dst, sems.at[1, i]).wait()
 
 
 def layer_call(positions, topk_ids, gains, big):
@@ -584,22 +664,22 @@
     freq = np.zeros((8, LANES), np.float32)
     freq[0, :ROPE_DIM] = np.tile((ROPE_BASE ** (-np.arange(half) / half)).astype(np.float32), 2)
     freq[1, :ROPE_DIM] = np.repeat([-1.0, 1.0], half)
-    vmem = pl.BlockSpec(memory_space=pltpu.VMEM)
     smem = pl.BlockSpec(memory_space=pltpu.SMEM)
     hbm = pl.BlockSpec(memory_space=pl.ANY)
     dma = pltpu.SemaphoreType.DMA
-    return pl.pallas_call(
+    shapes = [(tokens, width), (tokens, rank), (tokens, ROPE_DIM)]
+    outs = tuple(jax.ShapeDtypeStruct(shape, BF) for shape in shapes)
+    results = pl.pallas_call(
         layer_kernel,
-        out_shape=(jax.ShapeDtypeStruct((tokens, width), BF), jax.ShapeDtypeStruct((tokens, rank), BF),
-                   jax.ShapeDtypeStruct((tokens, ROPE_DIM), BF)),
-        in_specs=[smem] + [vmem] * 6 + [hbm] * len(big),
-        out_specs=(vmem, vmem, vmem),
-        scratch_shapes=[
+        out_shape=outs,
+        in_specs=[smem] + [hbm] * (6 + len(big)),
+        out_specs=(hbm, hbm, hbm),
+        scratch_shapes=[pltpu.VMEM(topk_ids.shape, jnp.int32), pltpu.VMEM(freq.shape, F4)]
+        + [pltpu.VMEM(g.shape, BF) for g in gains] + [pltpu.VMEM(shape, BF) for shape in shapes] + [
             pltpu.VMEM((total, width), BF),
             pltpu.VMEM((total, LANES), F4),
             pltpu.VMEM((DEPTH_A, width, 2 * FF_TILE), BF),
             pltpu.VMEM((DEPTH_B, ff, COL_TILE), BF),
-            pltpu.VMEM((2, big[5].shape[0], KV_ROWS), BF),
             pltpu.VMEM(big[9].shape, BF),
             pltpu.VMEM(big[2].shape, BF),
             pltpu.VMEM((tokens, big[5].shape[0]), F4),
@@ -612,6 +692,8 @@
             pltpu.VMEM((tokens // SUB, HEADS, SUB, rank), F4),
             pltpu.VMEM((tokens, HEADS * VALUE_DIM), BF),
             pltpu.VMEM((tokens, ff), BF),
+            pltpu.VMEM((total, FF_TILE), BF),
+            pltpu.VMEM((2, total, 2 * FF_TILE), F4),
             pltpu.VMEM((2, total, ff), BF),
             pltpu.VMEM((4, tokens, width), F4),
             pltpu.VMEM((SIB_SLOTS, 4, tokens, COL_TILE), F4),
@@ -619,11 +701,19 @@
             pltpu.VMEM((tokens, width), F4),
             pltpu.VMEM((tokens, width), F4),
             pltpu.VMEM((tokens, width), F4),
-            dma((2, DEPTH_A)), dma((DEPTH_B,)), dma((2,)), dma((3,)),
-        ] + [dma((n_grp,))] * 6 + [dma((4,))] * 2 + [dma((8,))] * 2 + [dma((n_col,))] * 8,
+            dma((2, DEPTH_A)), dma((DEPTH_B,)), dma((12,)), dma((8,)), dma((8,)),
+        ] + [dma((n_grp,))] * 6 + [dma((4,))] * 4 + [dma((n_col,))] * 8,
         compiler_params=pltpu.CompilerParams(collective_id=0, has_side_effects=True, vmem_limit_bytes=67043328),
         name='decode_layer',
     )(positions, topk_ids, jnp.asarray(freq), *gains, *big)
+    return pl.pallas_call(
+        hand_on,
+        out_shape=outs,
+        in_specs=[hbm] * 3,
+        out_specs=(hbm, hbm, hbm),
+        scratch_shapes=[pltpu.VMEM(shape, BF) for shape in shapes] + [dma((2, 3))],
+        name='hand_on',
+    )(*results)
 
 
 def solution(mesh):

time: 132 us -> 120 us (0.909)
  Pallas kernels: 126 us -> 119 us
  local copies, waits for them, and re-layouts: 4.48 us -> 0 us
    pallas_call x1 -> x2, Pallas kernels: 126 us -> 119 us  [the longest x1 117 us: layer_call(): pl.pallas_call(layer_kernel, out_shape=outs, in_specs=[smem] + [hbm] * (6...]
    unnamed x3 -> x0, local copies, waits for them, and re-layouts: 4.48 us -> none
where the time goes in v3:
time: 120 us; the launch traced here: 119 us
  Pallas kernels  119 us (99%)
    pallas_call x1, Pallas kernels, layer_call(): pl.pallas_call(layer_kernel, out_shape=outs, in_specs=[smem] + [hbm] * (6...  117 us

profile of v3, /device:TPU:0, one launch (start us, length us, event | category | flops | bytes accessed | tf_op | source)
XLA Modules:
  0.0 119.5 jit_solution(6210329635988913792)
XLA Ops:
  0.6 116.8 %decode_layer.1 = (bf16[32,7168]{1,0:T(8,128)(2,1)}, bf16[32,512]{1,0:T(8,128)(2,1)}, bf16[32,64]{1,0:T(8,128)(2,1)}) custom-call(s32[32]{0:T(128)} %pos_ref.1, s32[8,32]{1,0:T(8,128)} %bitcast.9, f32[8,128]{1,0:T(8,128)} %constant.2.clone.freq, bf16[7168]{0:T(1024)(128)(2,1)} %ag.1, bf16[1536]{0:T(1024)(128)(2,1)} %qg.1, bf16[512]{0:T(512)(128)(2,1)} %kg.1, ...), custom_call_target="tpu_custom_call" | custom-call | tf_op jit(solution)/shard_map/decode_layer/pallas_call | solution.py:672
  117.5 1.8 %hand_on.1 = (bf16[32,7168]{1,0:T(8,128)(2,1)}, bf16[32,512]{1,0:T(8,128)(2,1)}, bf16[32,64]{1,0:T(8,128)(2,1)}) custom-call(bf16[32,7168]{1,0:T(8,128)(2,1)} %get-tuple-element.6.a, bf16[32,512]{1,0:T(8,128)(2,1)} %get-tuple-element.7.b, bf16[32,64]{1,0:T(8,128)(2,1)} %get-tuple-element.8.c), custom_call_target="tpu_custom_call" | custom-call | tf_op jit(solution)/shard_map/hand_on/pallas_call | solution.py:709

commit v4 on v3

--- a/solution.py
+++ b/solution.py
@@ -40,7 +40,7 @@
                  hidden, ckv, kpe, dq, uq, dkv, uk, uv, wo, router, sg, su, sd, wg, wu, wd,
                  out_hbm, cnew_hbm, knew_hbm,
                  topk_ref, freq_ref, ag_ref, qg_ref, kg_ref, fg_ref, out_ref, cnew_ref, knew_ref,
-                 U, WT, wA, wB, wR, kp, kvs, hid, xm, cq, QN, QA, QR, CTX, O, acts, part_s, H, ACT, Pm, Ps, R1, RL, RX, RY,
+                 U, WT, wA, wB, wR, kp, kvs, hid, xm, cq, QN, QA, QR, O, acts, part_s, H, ACT, Pm, Ps, R1, RL, RX, RY,
                  semA, semB, semM, as_s, as_r, px_s, px_r, py_s, py_r, pr_s, pr_r, d_s, d_r, w_s, w_r,
                  sib_s, sib_r, rl_s, rl_r, x_s, x_r, y_s, y_r):
     tokens, width = hid.shape
@@ -264,7 +264,6 @@
         return carry
 
     lax.fori_loop(0, n_q // 2, uq_step, 0)
-    issueA(jnp.int32(n_dq))
 
     cnew_ref[...] = rms(kvs[:, 0:rank], gain(kg_ref)).astype(BF)
     knew_ref[...] = rotate(kvs[:, rank:rank + ROPE_DIM]).astype(BF)
@@ -308,14 +307,14 @@
         p = (e / denom).astype(BF)
         p_self = (e_self / denom).astype(BF).astype(F4)
         ctx = dot(p.reshape(HEADS * SUB, span), keys).reshape(HEADS, SUB, rank) + p_self * cn[None]
-        CTX[g] = ctx.astype(BF).astype(F4)
+        QA[g] = ctx.astype(BF).astype(F4)
     issueB(jnp.int32(B_CKV + DEPTH_B))
 
     waitB(B_UV)
     slot_uv = B_UV % DEPTH_B
     for h in range(HEADS):
         w_h = wB[slot_uv, (h // 4) * rank:(h // 4 + 1) * rank, (h % 4) * VALUE_DIM:(h % 4 + 1) * VALUE_DIM]
-        O[:, h * VALUE_DIM:(h + 1) * VALUE_DIM] = dot(CTX[:, h].reshape(tokens, rank).astype(BF), w_h).astype(BF)
+        O[:, h * VALUE_DIM:(h + 1) * VALUE_DIM] = dot(QA[:, h].reshape(tokens, rank).astype(BF), w_h).astype(BF)
     issueB(jnp.int32(B_UV + DEPTH_B))
 
     pl.semaphore_wait(barrier, 7)
@@ -375,9 +374,9 @@
             forward(2 * (i - PASS_LAG))
             forward(2 * (i - PASS_LAG) + 1)
 
-        @pl.when((i >= A_AT) & (i < A_AT + DEPTH_A - 1))
-        def _():
-            issueA(i - A_AT + n_dq + 1)
+        @pl.when((i >= A_AT) & (i < A_AT + DEPTH_A))
+        def _():
+            issueA(i - A_AT + n_dq)
         return carry
 
     lax.fori_loop(0, n_col // 2, out_step, 0)
@@ -460,6 +459,8 @@
     to_twin(3, kD).start()
     wait_pair(A_S0)
     part_s[0:4 * tokens, :] = gated(dot(U[0:4 * tokens, :], wA[A_S0 % DEPTH_A]))
+    wait_pair(A_R)
+    H[0, 0:4 * tokens, :] = dot(U[0:4 * tokens, :], wA[A_R % DEPTH_A])
     for i, k, dev in mates:
         table_from(i, k, dev).wait_recv()
     tables_to_twin().start()
@@ -468,6 +469,8 @@
         rcopy(U.at[rows(k), :], U.at[rows(4 + k), :], d_s.at[i], d_r.at[i], sib).wait_recv()
     part_s[4 * tokens:8 * tokens, :] = gated(dot(U[4 * tokens:8 * tokens, :], wA[A_S0 % DEPTH_A]))
     issueA(jnp.int32(A_S0 + DEPTH_A))
+    H[0, 4 * tokens:8 * tokens, :] = dot(U[4 * tokens:8 * tokens, :], wA[A_R % DEPTH_A])
+    issueA(jnp.int32(A_R + DEPTH_A))
     toS.wait_send()
     for i, k in ((1, kX), (2, kY), (3, kD)):
         to_twin(i, k).wait_send()
@@ -497,9 +500,6 @@
         issueA(t + DEPTH_A)
         return carry
 
-    wait_pair(A_R)
-    H[0] = dot(U[...], wA[A_R % DEPTH_A])
-    issueA(jnp.int32(A_R + DEPTH_A))
     lax.fori_loop(1, 2 * n_ff, routed_up_step, 0)
     ACT[1, :, ff - FF_TILE:ff] = gated(H[(2 * n_ff - 1) % 2])
 
@@ -689,7 +689,6 @@
             pltpu.VMEM((HEADS, tokens, NOPE_DIM), BF),
             pltpu.VMEM((tokens // SUB, HEADS, SUB, rank), F4),
             pltpu.VMEM((tokens // SUB, HEADS, SUB, ROPE_DIM), F4),
-            pltpu.VMEM((tokens // SUB, HEADS, SUB, rank), F4),
             pltpu.VMEM((tokens, HEADS * VALUE_DIM), BF),
             pltpu.VMEM((tokens, ff), BF),
             pltpu.VMEM((total, FF_TILE), BF),

time: 120 us -> 119 us (level)
  no operation moved by 1% of the time
where the time goes in v4:
time: 119 us
  Pallas kernels  118 us (99%)
    pallas_call x1, Pallas kernels, layer_call(): pl.pallas_call(layer_kernel, out_shape=outs, in_specs=[smem] + [hbm] * (6...  116 us

profile of v4, /device:TPU:0, one launch (start us, length us, event | category | flops | bytes accessed | tf_op | source)
XLA Modules:
  0.0 118.9 jit_solution(2428667488245683568)
XLA Ops:
  0.6 116.2 %decode_layer.1 = (bf16[32,7168]{1,0:T(8,128)(2,1)}, bf16[32,512]{1,0:T(8,128)(2,1)}, bf16[32,64]{1,0:T(8,128)(2,1)}) custom-call(s32[32]{0:T(128)} %pos_ref.1, s32[8,32]{1,0:T(8,128)} %bitcast.9, f32[8,128]{1,0:T(8,128)} %constant.2.clone.freq, bf16[7168]{0:T(1024)(128)(2,1)} %ag.1, bf16[1536]{0:T(1024)(128)(2,1)} %qg.1, bf16[512]{0:T(512)(128)(2,1)} %kg.1, ...), custom_call_target="tpu_custom_call" | custom-call | tf_op jit(solution)/shard_map/decode_layer/pallas_call | solution.py:672
  116.9 1.8 %hand_on.1 = (bf16[32,7168]{1,0:T(8,128)(2,1)}, bf16[32,512]{1,0:T(8,128)(2,1)}, bf16[32,64]{1,0:T(8,128)(2,1)}) custom-call(bf16[32,7168]{1,0:T(8,128)(2,1)} %get-tuple-element.6.a, bf16[32,512]{1,0:T(8,128)(2,1)} %get-tuple-element.7.b, bf16[32,64]{1,0:T(8,128)(2,1)} %get-tuple-element.8.c), custom_call_target="tpu_custom_call" | custom-call | tf_op jit(solution)/shard_map/hand_on/pallas_call | solution.py:708
